TPU v7x, 1024 devices: a whole 4x8x16 slice. The times are simulated.
1024 devices in a mesh: gx: 16 (over z_lo, x), gy: 64 (over z_hi, y, core).
Axes of the slice: x: 4, y: 8, z: 16 (z_hi: 4, z_lo: 4; z = z_hi * 4 + z_lo), core: 2. Of those that a mesh axis runs over, the one named last changes fastest.
Arguments:
- velocity: float32 [3, 512, 512, 128], P(None, 'gx', 'gy'), may hold values from -6 to 6
- stress: float32 [6, 512, 512, 128], P(None, 'gx', 'gy'), may hold values from -6 to 6
- lame_first: float32 [512, 512, 128], P('gx', 'gy'), may hold values from 0.5 to 2
- modulus: float32 [512, 512, 128], P('gx', 'gy'), may hold values from 0.5 to 2
- buoyancy: float32 [512, 512, 128], P('gx', 'gy'), may hold values from 0.5 to 2
- zone: int32 [512, 512, 128], P('gx', 'gy'), may hold values from 0 to 7
- eligible: int32 [512, 512, 128], P('gx', 'gy'), may hold values 0 or 1
- cohesion: float32 [8], replicated, may hold values from 0.2 to 2
- friction: float32 [8], replicated, may hold values from 0.1 to 0.6
- source_cell: int32 [16], replicated, may hold values from 0 to 33554431
- source_moment: float32 [6, 16], replicated, may hold values from -15 to 15
Outputs:
- velocity_out: float32 [3, 512, 512, 128], P(None, 'gx', 'gy')
- stress_out: float32 [6, 512, 512, 128], P(None, 'gx', 'gy')
All inputs are finite; a program needn't handle non-finite values. No bound on the sum of `eligible` on one device may be relied on, other than what follows from the above.
Results may differ from a plain program's by a relative error of at most 0.00011.
Values sent between devices are 32-bit elements; how exact they have to be, the bound alone decides.
A program may use at most 32 MiB of HBM per device.

v0:
```python
import jax
import jax.numpy as jnp
from jax import lax
from jax.sharding import PartitionSpec as P

STEPS = 2


time_step = 0.1
near_weight = 9.0 / 8.0
far_weight = 1.0 / 24.0
shear_floor = 0.25


def extended(block, sides, width):
    for axis, dim in sides:
        count = lax.axis_size(axis)
        forward = [(i, i + 1) for i in range(count - 1)]
        backward = [(target, source) for source, target in forward]
        low = lax.ppermute(
            lax.slice_in_dim(block, block.shape[dim] - width, None, axis=dim), axis, forward
        )
        high = lax.ppermute(lax.slice_in_dim(block, 0, width, axis=dim), axis, backward)
        block = jnp.concatenate([low, block, high], axis=dim)
    return block


def padded_2(shard, sides, width):
    edges = {}
    for axis, dim in sides:
        devices, length = (lax.axis_size(axis), shard.shape[dim])
        up = [(i, (i + 1) % devices) for i in range(devices - 1)]
        last = lax.slice_in_dim(shard, length - width, length, axis=dim)
        leading = lax.slice_in_dim(shard, 0, width, axis=dim)
        edges[dim] = (
            lax.ppermute(last, axis, up),
            lax.ppermute(leading, axis, [(b, a) for a, b in up]),
        )
    done = []
    for _, dim in sides:
        low, high = edges[dim]
        around = [(width, width) if d in done else (0, 0) for d in range(shard.ndim)]
        shard = jnp.concatenate([jnp.pad(low, around), shard, jnp.pad(high, around)], axis=dim)
        done.append(dim)
    return shard


def crop(padded, axis, offset):
    result = padded
    for dim in range(3):
        begin = offset if dim == axis else 2
        length = padded.shape[dim] - 4
        result = lax.slice_in_dim(result, begin, begin + length, axis=dim)
    return result


def derivative(padded, axis, forward):
    if forward:
        return near_weight * (crop(padded, axis, 3) - crop(padded, axis, 2)) - far_weight * (
            crop(padded, axis, 4) - crop(padded, axis, 1)
        )
    return near_weight * (crop(padded, axis, 2) - crop(padded, axis, 1)) - far_weight * (
        crop(padded, axis, 3) - crop(padded, axis, 0)
    )


def split_velocity_update(along_x, along_y, along_z, velocity, buoyancy):
    force_x = (
        derivative(along_x[0], 0, True)
        + derivative(along_y[0], 1, False)
        + derivative(along_z[0], 2, False)
    )
    force_y = (
        derivative(along_x[1], 0, False)
        + derivative(along_y[1], 1, True)
        + derivative(along_z[1], 2, False)
    )
    force_z = (
        derivative(along_x[2], 0, False)
        + derivative(along_y[2], 1, False)
        + derivative(along_z[2], 2, True)
    )
    forces = jnp.stack([force_x, force_y, force_z])
    return velocity + time_step * buoyancy[None] * forces


def stress_update(flow_pad, stress, lame_first, modulus):
    strain_x = derivative(flow_pad[0], 0, False)
    strain_y = derivative(flow_pad[1], 1, False)
    strain_z = derivative(flow_pad[2], 2, False)
    dilation = strain_x + strain_y + strain_z
    shear_xy = derivative(flow_pad[0], 1, True) + derivative(flow_pad[1], 0, True)
    shear_xz = derivative(flow_pad[0], 2, True) + derivative(flow_pad[2], 0, True)
    shear_yz = derivative(flow_pad[1], 2, True) + derivative(flow_pad[2], 1, True)
    rates = jnp.stack(
        [
            lame_first * dilation + 2.0 * modulus * strain_x,
            lame_first * dilation + 2.0 * modulus * strain_y,
            lame_first * dilation + 2.0 * modulus * strain_z,
            modulus * shear_xy,
            modulus * shear_xz,
            modulus * shear_yz,
        ]
    )
    return stress + time_step * rates


def plastic(stress, cell_cohesion, cell_friction, eligible):
    pressure = (stress[0] + stress[1] + stress[2]) / 3.0
    dev_x = stress[0] - pressure
    dev_y = stress[1] - pressure
    dev_z = stress[2] - pressure
    second = (
        0.5 * (dev_x * dev_x + dev_y * dev_y + dev_z * dev_z)
        + stress[3] * stress[3]
        + stress[4] * stress[4]
        + stress[5] * stress[5]
    )
    strength = jnp.maximum(
        cell_cohesion * jnp.sqrt(1.0 - cell_friction * cell_friction) - pressure * cell_friction,
        0.0,
    )
    ratio = jnp.minimum(1.0, strength / jnp.maximum(jnp.sqrt(second), shear_floor))
    factor = jnp.where(eligible == 1, ratio, 1.0)
    return jnp.stack(
        [
            pressure + factor * dev_x,
            pressure + factor * dev_y,
            pressure + factor * dev_z,
            factor * stress[3],
            factor * stress[4],
            factor * stress[5],
        ]
    )


def pad_depth(field, width):
    return jnp.pad(field, ((0, 0), (0, 0), (0, 0), (width, width)))


def on_device(
    velocity,
    stress,
    lame_first,
    modulus,
    buoyancy,
    zone,
    eligible,
    cohesion,
    friction,
    source_cell,
    source_moment,
):
    rows_x, rows_y, depth = zone.shape
    total_y = rows_y * lax.axis_size("gy")
    start_x = lax.axis_index("gx") * rows_x
    start_y = lax.axis_index("gy") * rows_y
    cell_cohesion = jnp.zeros(zone.shape, jnp.float32)
    cell_friction = jnp.zeros(zone.shape, jnp.float32)
    for which in range(cohesion.shape[0]):
        hit = zone == which
        cell_cohesion = cell_cohesion + jnp.where(hit, cohesion[which], 0.0)
        cell_friction = cell_friction + jnp.where(hit, friction[which], 0.0)
    plane = total_y * depth
    src_x = source_cell // plane
    src_y = source_cell // depth % total_y
    src_z = source_cell % depth
    pick_x = (src_x[:, None] == start_x + jnp.arange(rows_x, dtype=jnp.int32)[None]).astype(
        jnp.float32
    )
    pick_y = (src_y[:, None] == start_y + jnp.arange(rows_y, dtype=jnp.int32)[None]).astype(
        jnp.float32
    )
    pick_z = (src_z[:, None] == jnp.arange(depth, dtype=jnp.int32)[None]).astype(jnp.float32)
    injection = jnp.einsum(
        "cs,sx,sy,sz->cxyz",
        time_step * source_moment,
        pick_x,
        pick_y,
        pick_z,
        precision=lax.Precision.HIGHEST,
    )
    for step in range(STEPS):
        strike_part = jnp.stack([stress[0], stress[3], stress[4]])
        normal_part = jnp.stack([stress[3], stress[1], stress[5]])
        depth_part = jnp.stack([stress[4], stress[5], stress[2]])
        along_x = extended(strike_part, (("gx", 1),), 2)
        along_y = extended(normal_part, (("gy", 2),), 2)
        along_x = jnp.pad(along_x, ((0, 0), (0, 0), (2, 2), (2, 2)))
        along_y = jnp.pad(along_y, ((0, 0), (2, 2), (0, 0), (2, 2)))
        along_z = jnp.pad(depth_part, ((0, 0), (2, 2), (2, 2), (2, 2)))
        velocity = split_velocity_update(along_x, along_y, along_z, velocity, buoyancy)
        flow_pad = padded_2(velocity, (("gx", 1), ("gy", 2)), 2)
        stress = stress_update(pad_depth(flow_pad, 2), stress, lame_first, modulus)
        stress = stress + injection
        stress = plastic(stress, cell_cohesion, cell_friction, eligible)
    return (velocity, stress)


def solution(mesh):
    placed = (
        P(None, "gx", "gy", None),
        P(None, "gx", "gy", None),
        P("gx", "gy", None),
        P("gx", "gy", None),
        P("gx", "gy", None),
        P("gx", "gy", None),
        P("gx", "gy", None),
        P(),
        P(),
        P(),
        P(),
    )
    return jax.shard_map(
        on_device,
        mesh=mesh,
        in_specs=placed,
        out_specs=(P(None, "gx", "gy", None), P(None, "gx", "gy", None)),
        check_vma=False,
    )
```

profile of v0, /device:TPU:127, one launch (start us, length us, event | category | flops | bytes accessed | tf_op | source)
XLA Modules:
  0.0 136.1 jit_solution(4440714279480020248)
XLA Ops:
  0.6 1.1 fusion.207
  2.1 3.9 %collective-permute-start = (f32[3,2,8,128]{3,1,2,0:T(2,128)S(1)}, f32[3,2,8,128]{3,1,2,0:T(2,128)S(1)}, u32[]{:S(2)}, u32[]{:S(2)}) collective-permute-start(f32[3,2,8,128]{3,1,2,0:T(2,128)S(1)} %get-tuple-element.117), channel_id=1, source_target_pairs={{0,64},{64,128},{128,192},{192,256},{256,320},{320,384},{384,448},... | collective-permute-start | bytes 73736 | tf_op jit(solution)/shard_map/ppermute | solution.py:20
  6.0 1.9 %collective-permute-start.1 = (f32[3,2,8,128]{3,1,2,0:T(2,128)S(1)}, f32[3,2,8,128]{3,1,2,0:T(2,128)S(1)}, u32[]{:S(2)}, u32[]{:S(2)}) collective-permute-start(f32[3,2,8,128]{3,1,2,0:T(2,128)S(1)} %get-tuple-element.118), channel_id=1, source_target_pairs={{64,0},{128,64},{192,128},{256,192},{320,256},{384,320},{448,384},... | collective-permute-start | bytes 73736 | tf_op jit(solution)/shard_map/ppermute | solution.py:23
  8.1 10.7 %collective-permute-start.2 = (f32[3,32,2,128]{3,1,2,0:T(8,128)S(1)}, f32[3,32,2,128]{3,1,2,0:T(8,128)S(1)}, u32[]{:S(2)}, u32[]{:S(2)}) collective-permute-start(f32[3,32,2,128]{3,1,2,0:T(8,128)S(1)} %get-tuple-element.119), channel_id=1, source_target_pairs={{0,1},{1,2},{2,3},{3,4},{4,5},{5,6},{6,7},{7,8},{8,9},{9,10},{10,1... | collective-permute-start | bytes 294920 | tf_op jit(solution)/shard_map/ppermute | solution.py:20
  18.8 1.9 %collective-permute-start.3 = (f32[3,32,2,128]{3,1,2,0:T(8,128)S(1)}, f32[3,32,2,128]{3,1,2,0:T(8,128)S(1)}, u32[]{:S(2)}, u32[]{:S(2)}) collective-permute-start(f32[3,32,2,128]{3,1,2,0:T(8,128)S(1)} %get-tuple-element.120), channel_id=1, source_target_pairs={{1,0},{2,1},{3,2},{4,3},{5,4},{6,5},{7,6},{8,7},{9,8},{10,9},{11,1... | collective-permute-start | bytes 294920 | tf_op jit(solution)/shard_map/ppermute | solution.py:23
  21.6 1.0 convolution_bitcast_fusion
  22.6 0.7 fusion.212
  24.5 6.3 %collective-permute-done.3 = f32[3,32,2,128]{3,1,2,0:T(8,128)S(1)} collective-permute-done((f32[3,32,2,128]{3,1,2,0:T(8,128)S(1)}, f32[3,32,2,128]{3,1,2,0:T(8,128)S(1)}, u32[]{:S(2)}, u32[]{:S(2)}) %collective-permute-start.3) | collective-permute-done | bytes 98336 | tf_op jit(solution)/shard_map/ppermute | solution.py:23
  33.0 5.8 %collective-permute-start.5 = (f32[3,2,8,128]{3,1,2,0:T(2,128)S(1)}, f32[3,2,8,128]{3,1,2,0:T(2,128)S(1)}, u32[]{:S(2)}, u32[]{:S(2)}) collective-permute-start(f32[3,2,8,128]{3,1,2,0:T(2,128)S(1)} %get-tuple-element.113), channel_id=1, source_target_pairs={{0,64},{64,128},{128,192},{192,256},{256,320},{320,384},{384,448},... | collective-permute-start | bytes 73736 | tf_op jit(solution)/shard_map/ppermute | solution.py:36
  38.8 1.9 %collective-permute-start.6 = (f32[3,2,8,128]{3,1,2,0:T(2,128)S(1)}, f32[3,2,8,128]{3,1,2,0:T(2,128)S(1)}, u32[]{:S(2)}, u32[]{:S(2)}) collective-permute-start(f32[3,2,8,128]{3,1,2,0:T(2,128)S(1)} %get-tuple-element.114), channel_id=1, source_target_pairs={{64,0},{128,64},{192,128},{256,192},{320,256},{384,320},{448,384},... | collective-permute-start | bytes 73736 | tf_op jit(solution)/shard_map/ppermute | solution.py:37
  40.7 3.6 %collective-permute-start.4 = (f32[3,32,2,128]{3,1,2,0:T(8,128)S(1)}, f32[3,32,2,128]{3,1,2,0:T(8,128)S(1)}, u32[]{:S(2)}, u32[]{:S(2)}) collective-permute-start(f32[3,32,2,128]{3,1,2,0:T(8,128)S(1)} %get-tuple-element.115), channel_id=1, source_target_pairs={{0,1},{1,2},{2,3},{3,4},{4,5},{5,6},{6,7},{7,8},{8,9},{9,10},{10,1... | collective-permute-start | bytes 294920 | tf_op jit(solution)/shard_map/ppermute | solution.py:36
  44.3 1.9 %collective-permute-start.7 = (f32[3,32,2,128]{3,1,2,0:T(8,128)S(1)}, f32[3,32,2,128]{3,1,2,0:T(8,128)S(1)}, u32[]{:S(2)}, u32[]{:S(2)}) collective-permute-start(f32[3,32,2,128]{3,1,2,0:T(8,128)S(1)} %get-tuple-element.116), channel_id=1, source_target_pairs={{1,0},{2,1},{3,2},{4,3},{5,4},{6,5},{7,6},{8,7},{9,8},{10,9},{11,1... | collective-permute-start | bytes 294920 | tf_op jit(solution)/shard_map/ppermute | solution.py:37
  46.3 0.7 fusion.213
  47.0 9.3 %collective-permute-done.7 = f32[3,32,2,128]{3,1,2,0:T(8,128)S(1)} collective-permute-done((f32[3,32,2,128]{3,1,2,0:T(8,128)S(1)}, f32[3,32,2,128]{3,1,2,0:T(8,128)S(1)}, u32[]{:S(2)}, u32[]{:S(2)}) %collective-permute-start.7) | collective-permute-done | bytes 98336 | tf_op jit(solution)/shard_map/ppermute | solution.py:37
  56.4 1.3 fusion.19
  60.3 10.6 %constant_dynamic-update-slice_fusion.5 = (f32[6,32,8,128]{3,1,2,0:T(8,128)S(1)}, f32[1,32,8,128]{3,1,2,0:T(8,128)S(1)}, f32[32,8,128]{2,0,1:T(8,128)S(1)}, pred...) fusion(f32[6,32,8,128]{3,1,2,0:T(8,128)S(1)} %copy_add_fusion.1, ...), kind=kLoop, calls=%fused_computation.422 | loop fusion | flops 2260991 | bytes 1867840
  71.1 1.9 %collective-permute-start.10 = (f32[3,32,2,128]{3,1,2,0:T(8,128)S(1)}, f32[3,32,2,128]{3,1,2,0:T(8,128)S(1)}, u32[]{:S(2)}, u32[]{:S(2)}) collective-permute-start(f32[3,32,2,128]{3,1,2,0:T(8,128)S(1)} %get-tuple-element.111), channel_id=1, source_target_pairs={{0,1},{1,2},{2,3},{3,4},{4,5},{5,6},{6,7},{7,8},{8,9},{9,10},{10,1... | collective-permute-start | bytes 294920 | tf_op jit(solution)/shard_map/ppermute | solution.py:20
  73.0 2.4 %collective-permute-start.11 = (f32[3,32,2,128]{3,1,2,0:T(8,128)S(1)}, f32[3,32,2,128]{3,1,2,0:T(8,128)S(1)}, u32[]{:S(2)}, u32[]{:S(2)}) collective-permute-start(f32[3,32,2,128]{3,1,2,0:T(8,128)S(1)} %get-tuple-element.112), channel_id=1, source_target_pairs={{1,0},{2,1},{3,2},{4,3},{5,4},{6,5},{7,6},{8,7},{9,8},{10,9},{11,1... | collective-permute-start | bytes 294920 | tf_op jit(solution)/shard_map/ppermute | solution.py:23
  75.5 7.9 %collective-permute-start.8 = (f32[3,2,8,128]{3,1,2,0:T(2,128)S(1)}, f32[3,2,8,128]{3,1,2,0:T(2,128)S(1)}, u32[]{:S(2)}, u32[]{:S(2)}) collective-permute-start(f32[3,2,8,128]{3,1,2,0:T(2,128)S(1)} %get-tuple-element.109), channel_id=1, source_target_pairs={{0,64},{64,128},{128,192},{192,256},{256,320},{320,384},{384,448},... | collective-permute-start | bytes 73736 | tf_op jit(solution)/shard_map/ppermute | solution.py:20
  83.3 2.1 %collective-permute-start.9 = (f32[3,2,8,128]{3,1,2,0:T(2,128)S(1)}, f32[3,2,8,128]{3,1,2,0:T(2,128)S(1)}, u32[]{:S(2)}, u32[]{:S(2)}) collective-permute-start(f32[3,2,8,128]{3,1,2,0:T(2,128)S(1)} %get-tuple-element.110), channel_id=1, source_target_pairs={{64,0},{128,64},{192,128},{256,192},{320,256},{384,320},{448,384},... | collective-permute-start | bytes 73736 | tf_op jit(solution)/shard_map/ppermute | solution.py:23
  85.4 4.6 %collective-permute-done.9 = f32[3,2,8,128]{3,1,2,0:T(2,128)S(1)} collective-permute-done((f32[3,2,8,128]{3,1,2,0:T(2,128)S(1)}, f32[3,2,8,128]{3,1,2,0:T(2,128)S(1)}, u32[]{:S(2)}, u32[]{:S(2)}) %collective-permute-start.9) | collective-permute-done | bytes 24608 | tf_op jit(solution)/shard_map/ppermute | solution.py:23
  90.0 3.8 %select_maximum_fusion.6 = (f32[3,36,12,132]{3,1,2,0:T(8,128)S(1)}, f32[3,36,12,132]{3,1,2,0:T(8,128)S(1)}, f32[3,36,12,132]{3,1,2,0:T(8,128)S(1)}) fusion(f32[3,2,8,128]{3,1,2,0:T(2,128)S(1)} %collective-permute-done.9, f32[3,2,8,128]{3,1,2,0:T(2,128)S(1)} %collective-permute-done.8, f32[1,32,8,128]{3,1,2,0:T(8,128)S(1)} %get-tuple-element.14, ...), kind=kLoop, calls=%fused_computation.45 | loop fusion | flops 9408960 | bytes 3085056 | tf_op jit(solution)/shard_map/concatenate | solution.py:24
  96.4 11.6 %collective-permute-start.12 = (f32[3,32,2,128]{3,1,2,0:T(8,128)S(1)}, f32[3,32,2,128]{3,1,2,0:T(8,128)S(1)}, u32[]{:S(2)}, u32[]{:S(2)}) collective-permute-start(f32[3,32,2,128]{3,1,2,0:T(8,128)S(1)} %get-tuple-element.107), channel_id=1, source_target_pairs={{0,1},{1,2},{2,3},{3,4},{4,5},{5,6},{6,7},{7,8},{8,9},{9,10},{10,1... | collective-permute-start | bytes 294920 | tf_op jit(solution)/shard_map/ppermute | solution.py:36
  107.9 1.9 %collective-permute-start.15 = (f32[3,32,2,128]{3,1,2,0:T(8,128)S(1)}, f32[3,32,2,128]{3,1,2,0:T(8,128)S(1)}, u32[]{:S(2)}, u32[]{:S(2)}) collective-permute-start(f32[3,32,2,128]{3,1,2,0:T(8,128)S(1)} %get-tuple-element.108), channel_id=1, source_target_pairs={{1,0},{2,1},{3,2},{4,3},{5,4},{6,5},{7,6},{8,7},{9,8},{10,9},{11,1... | collective-permute-start | bytes 294920 | tf_op jit(solution)/shard_map/ppermute | solution.py:37
  109.9 1.9 %collective-permute-start.13 = (f32[3,2,8,128]{3,1,2,0:T(2,128)S(1)}, f32[3,2,8,128]{3,1,2,0:T(2,128)S(1)}, u32[]{:S(2)}, u32[]{:S(2)}) collective-permute-start(f32[3,2,8,128]{3,1,2,0:T(2,128)S(1)} %get-tuple-element.105), channel_id=1, source_target_pairs={{0,64},{64,128},{128,192},{192,256},{256,320},{320,384},{384,448},... | collective-permute-start | bytes 73736 | tf_op jit(solution)/shard_map/ppermute | solution.py:36
  111.8 3.4 %collective-permute-start.14 = (f32[3,2,8,128]{3,1,2,0:T(2,128)S(1)}, f32[3,2,8,128]{3,1,2,0:T(2,128)S(1)}, u32[]{:S(2)}, u32[]{:S(2)}) collective-permute-start(f32[3,2,8,128]{3,1,2,0:T(2,128)S(1)} %get-tuple-element.106), channel_id=1, source_target_pairs={{64,0},{128,64},{192,128},{256,192},{320,256},{384,320},{448,384},... | collective-permute-start | bytes 73736 | tf_op jit(solution)/shard_map/ppermute | solution.py:37
  115.2 1.0 copy.48
  116.2 2.3 %collective-permute-done.14 = f32[3,2,8,128]{3,1,2,0:T(2,128)S(1)} collective-permute-done((f32[3,2,8,128]{3,1,2,0:T(2,128)S(1)}, f32[3,2,8,128]{3,1,2,0:T(2,128)S(1)}, u32[]{:S(2)}, u32[]{:S(2)}) %collective-permute-start.14) | collective-permute-done | bytes 24608 | tf_op jit(solution)/shard_map/ppermute | solution.py:37
  118.5 2.4 %collective-permute-done.15 = f32[3,32,2,128]{3,1,2,0:T(8,128)S(1)} collective-permute-done((f32[3,32,2,128]{3,1,2,0:T(8,128)S(1)}, f32[3,32,2,128]{3,1,2,0:T(8,128)S(1)}, u32[]{:S(2)}, u32[]{:S(2)}) %collective-permute-start.15) | collective-permute-done | bytes 98336 | tf_op jit(solution)/shard_map/ppermute | solution.py:37
  121.0 1.3 fusion.31
  124.1 10.5 %bitcast_dynamic-update-slice_fusion.5 = (f32[6,32,8,128]{3,1,2,0:T(8,128)S(1)}, f32[32,8,128]{2,0,1:T(8,128)S(1)}, f32[32,8,128]{2,0,1:T(8,128)S(1)}) fusion(f32[6,32,8,128]{3,1,0,2:T(8,128)S(1)} %copy_add_fusion, pred[32,8,128]{2,0,1:T(8,128)(4,1)S(1)} %get-tuple-element.32, pred[32,8,128]{2,0,1:T(8,128)(4,1)S(1)} %get-tuple-element.31, f32[]{:T(128)} %bitcast.62, ...), kind=kLoop, calls=%fused_computation.371 | loop fusion | flops 1966079 | bytes 1474624
  134.8 1.3 copy.49
  (100 shorter events, 11.9 us)
Async XLA Ops:
  0.6 1.3 copy-start.1
  2.0 18.8 %copy-start.10 = (s32[16]{0:T(128)S(1)}, s32[16]{0:T(128)}, u32[]{:S(2)}) copy-start(s32[16]{0:T(128)} %param.20) | copy-start | bytes 196
  2.0 18.8 %copy-start.9 = (f32[6,16]{1,0:T(8,128)S(1)}, f32[6,16]{1,0:T(8,128)}, u32[]{:S(2)}) copy-start(f32[6,16]{1,0:T(8,128)} %param.21) | copy-start | bytes 1156
  2.0 18.9 %copy-start.6 = (f32[32,8,128]{2,1,0:T(8,128)S(1)}, f32[32,8,128]{2,1,0:T(8,128)}, u32[]{:S(2)}) copy-start(f32[32,8,128]{2,1,0:T(8,128)} %param.15) | copy-start | bytes 393220
  2.1 21.2 %collective-permute-start = (f32[3,2,8,128]{3,1,2,0:T(2,128)S(1)}, f32[3,2,8,128]{3,1,2,0:T(2,128)S(1)}, u32[]{:S(2)}, u32[]{:S(2)}) collective-permute-start(f32[3,2,8,128]{3,1,2,0:T(2,128)S(1)} %get-tuple-element.117), channel_id=1, source_target_pairs={{0,64},{64,128},{128,192},{192,256},{256,320},{320,384},{384,448},... | collective-permute-start | bytes 73736 | tf_op jit(solution)/shard_map/ppermute | solution.py:20
  6.0 17.3 %collective-permute-start.1 = (f32[3,2,8,128]{3,1,2,0:T(2,128)S(1)}, f32[3,2,8,128]{3,1,2,0:T(2,128)S(1)}, u32[]{:S(2)}, u32[]{:S(2)}) collective-permute-start(f32[3,2,8,128]{3,1,2,0:T(2,128)S(1)} %get-tuple-element.118), channel_id=1, source_target_pairs={{64,0},{128,64},{192,128},{256,192},{320,256},{384,320},{448,384},... | collective-permute-start | bytes 73736 | tf_op jit(solution)/shard_map/ppermute | solution.py:23
  8.1 16.3 %collective-permute-start.2 = (f32[3,32,2,128]{3,1,2,0:T(8,128)S(1)}, f32[3,32,2,128]{3,1,2,0:T(8,128)S(1)}, u32[]{:S(2)}, u32[]{:S(2)}) collective-permute-start(f32[3,32,2,128]{3,1,2,0:T(8,128)S(1)} %get-tuple-element.119), channel_id=1, source_target_pairs={{0,1},{1,2},{2,3},{3,4},{4,5},{5,6},{6,7},{7,8},{8,9},{9,10},{10,1... | collective-permute-start | bytes 294920 | tf_op jit(solution)/shard_map/ppermute | solution.py:20
  18.8 12.0 %collective-permute-start.3 = (f32[3,32,2,128]{3,1,2,0:T(8,128)S(1)}, f32[3,32,2,128]{3,1,2,0:T(8,128)S(1)}, u32[]{:S(2)}, u32[]{:S(2)}) collective-permute-start(f32[3,32,2,128]{3,1,2,0:T(8,128)S(1)} %get-tuple-element.120), channel_id=1, source_target_pairs={{1,0},{2,1},{3,2},{4,3},{5,4},{6,5},{7,6},{8,7},{9,8},{10,9},{11,1... | collective-permute-start | bytes 294920 | tf_op jit(solution)/shard_map/ppermute | solution.py:23
  21.3 1.3 copy-start.7
  31.8 1.0 copy-start.2
  32.3 14.0 %copy-start.8 = (f32[8]{0:T(128)S(1)}, f32[8]{0:T(128)}, u32[]{:S(2)}) copy-start(f32[8]{0:T(128)} %param.19) | copy-start | bytes 100
  33.0 14.0 %collective-permute-start.5 = (f32[3,2,8,128]{3,1,2,0:T(2,128)S(1)}, f32[3,2,8,128]{3,1,2,0:T(2,128)S(1)}, u32[]{:S(2)}, u32[]{:S(2)}) collective-permute-start(f32[3,2,8,128]{3,1,2,0:T(2,128)S(1)} %get-tuple-element.113), channel_id=1, source_target_pairs={{0,64},{64,128},{128,192},{192,256},{256,320},{320,384},{384,448},... | collective-permute-start | bytes 73736 | tf_op jit(solution)/shard_map/ppermute | solution.py:36
  38.8 8.1 %collective-permute-start.6 = (f32[3,2,8,128]{3,1,2,0:T(2,128)S(1)}, f32[3,2,8,128]{3,1,2,0:T(2,128)S(1)}, u32[]{:S(2)}, u32[]{:S(2)}) collective-permute-start(f32[3,2,8,128]{3,1,2,0:T(2,128)S(1)} %get-tuple-element.114), channel_id=1, source_target_pairs={{64,0},{128,64},{192,128},{256,192},{320,256},{384,320},{448,384},... | collective-permute-start | bytes 73736 | tf_op jit(solution)/shard_map/ppermute | solution.py:37
  40.7 6.2 %collective-permute-start.4 = (f32[3,32,2,128]{3,1,2,0:T(8,128)S(1)}, f32[3,32,2,128]{3,1,2,0:T(8,128)S(1)}, u32[]{:S(2)}, u32[]{:S(2)}) collective-permute-start(f32[3,32,2,128]{3,1,2,0:T(8,128)S(1)} %get-tuple-element.115), channel_id=1, source_target_pairs={{0,1},{1,2},{2,3},{3,4},{4,5},{5,6},{6,7},{7,8},{8,9},{9,10},{10,1... | collective-permute-start | bytes 294920 | tf_op jit(solution)/shard_map/ppermute | solution.py:36
  44.3 12.0 %collective-permute-start.7 = (f32[3,32,2,128]{3,1,2,0:T(8,128)S(1)}, f32[3,32,2,128]{3,1,2,0:T(8,128)S(1)}, u32[]{:S(2)}, u32[]{:S(2)}) collective-permute-start(f32[3,32,2,128]{3,1,2,0:T(8,128)S(1)} %get-tuple-element.116), channel_id=1, source_target_pairs={{1,0},{2,1},{3,2},{4,3},{5,4},{6,5},{7,6},{8,7},{9,8},{10,9},{11,1... | collective-permute-start | bytes 294920 | tf_op jit(solution)/shard_map/ppermute | solution.py:37
  56.4 1.3 copy-start
  56.4 1.3 copy-start.3
  59.3 0.9 copy-start.4
  59.4 1.0 copy-start.5
  71.1 18.9 %collective-permute-start.10 = (f32[3,32,2,128]{3,1,2,0:T(8,128)S(1)}, f32[3,32,2,128]{3,1,2,0:T(8,128)S(1)}, u32[]{:S(2)}, u32[]{:S(2)}) collective-permute-start(f32[3,32,2,128]{3,1,2,0:T(8,128)S(1)} %get-tuple-element.111), channel_id=1, source_target_pairs={{0,1},{1,2},{2,3},{3,4},{4,5},{5,6},{6,7},{7,8},{8,9},{9,10},{10,1... | collective-permute-start | bytes 294920 | tf_op jit(solution)/shard_map/ppermute | solution.py:20
  73.0 17.0 %collective-permute-start.11 = (f32[3,32,2,128]{3,1,2,0:T(8,128)S(1)}, f32[3,32,2,128]{3,1,2,0:T(8,128)S(1)}, u32[]{:S(2)}, u32[]{:S(2)}) collective-permute-start(f32[3,32,2,128]{3,1,2,0:T(8,128)S(1)} %get-tuple-element.112), channel_id=1, source_target_pairs={{1,0},{2,1},{3,2},{4,3},{5,4},{6,5},{7,6},{8,7},{9,8},{10,9},{11,1... | collective-permute-start | bytes 294920 | tf_op jit(solution)/shard_map/ppermute | solution.py:23
  75.5 10.0 %collective-permute-start.8 = (f32[3,2,8,128]{3,1,2,0:T(2,128)S(1)}, f32[3,2,8,128]{3,1,2,0:T(2,128)S(1)}, u32[]{:S(2)}, u32[]{:S(2)}) collective-permute-start(f32[3,2,8,128]{3,1,2,0:T(2,128)S(1)} %get-tuple-element.109), channel_id=1, source_target_pairs={{0,64},{64,128},{128,192},{192,256},{256,320},{320,384},{384,448},... | collective-permute-start | bytes 73736 | tf_op jit(solution)/shard_map/ppermute | solution.py:20
  83.3 6.7 %collective-permute-start.9 = (f32[3,2,8,128]{3,1,2,0:T(2,128)S(1)}, f32[3,2,8,128]{3,1,2,0:T(2,128)S(1)}, u32[]{:S(2)}, u32[]{:S(2)}) collective-permute-start(f32[3,2,8,128]{3,1,2,0:T(2,128)S(1)} %get-tuple-element.110), channel_id=1, source_target_pairs={{64,0},{128,64},{192,128},{256,192},{320,256},{384,320},{448,384},... | collective-permute-start | bytes 73736 | tf_op jit(solution)/shard_map/ppermute | solution.py:23
  96.4 22.1 %collective-permute-start.12 = (f32[3,32,2,128]{3,1,2,0:T(8,128)S(1)}, f32[3,32,2,128]{3,1,2,0:T(8,128)S(1)}, u32[]{:S(2)}, u32[]{:S(2)}) collective-permute-start(f32[3,32,2,128]{3,1,2,0:T(8,128)S(1)} %get-tuple-element.107), channel_id=1, source_target_pairs={{0,1},{1,2},{2,3},{3,4},{4,5},{5,6},{6,7},{7,8},{8,9},{9,10},{10,1... | collective-permute-start | bytes 294920 | tf_op jit(solution)/shard_map/ppermute | solution.py:36
  107.9 12.9 %collective-permute-start.15 = (f32[3,32,2,128]{3,1,2,0:T(8,128)S(1)}, f32[3,32,2,128]{3,1,2,0:T(8,128)S(1)}, u32[]{:S(2)}, u32[]{:S(2)}) collective-permute-start(f32[3,32,2,128]{3,1,2,0:T(8,128)S(1)} %get-tuple-element.108), channel_id=1, source_target_pairs={{1,0},{2,1},{3,2},{4,3},{5,4},{6,5},{7,6},{8,7},{9,8},{10,9},{11,1... | collective-permute-start | bytes 294920 | tf_op jit(solution)/shard_map/ppermute | solution.py:37
  109.9 6.3 %collective-permute-start.13 = (f32[3,2,8,128]{3,1,2,0:T(2,128)S(1)}, f32[3,2,8,128]{3,1,2,0:T(2,128)S(1)}, u32[]{:S(2)}, u32[]{:S(2)}) collective-permute-start(f32[3,2,8,128]{3,1,2,0:T(2,128)S(1)} %get-tuple-element.105), channel_id=1, source_target_pairs={{0,64},{64,128},{128,192},{192,256},{256,320},{320,384},{384,448},... | collective-permute-start | bytes 73736 | tf_op jit(solution)/shard_map/ppermute | solution.py:36
  111.8 6.7 %collective-permute-start.14 = (f32[3,2,8,128]{3,1,2,0:T(2,128)S(1)}, f32[3,2,8,128]{3,1,2,0:T(2,128)S(1)}, u32[]{:S(2)}, u32[]{:S(2)}) collective-permute-start(f32[3,2,8,128]{3,1,2,0:T(2,128)S(1)} %get-tuple-element.106), channel_id=1, source_target_pairs={{64,0},{128,64},{192,128},{256,192},{320,256},{384,320},{448,384},... | collective-permute-start | bytes 73736 | tf_op jit(solution)/shard_map/ppermute | solution.py:37
where the time goes:
time: 137 us; the launch traced here: 136 us
  starting transfers between devices  64.7 us (47%)
  other arithmetic  33.6 us (25%)
  waiting for transfers between devices  24.9 us (18%)
  local copies, waits for them, and re-layouts  10.5 us (8%)
  between operations  1.39 us (1%)
    ppermute x4, starting transfers between devices, extended(): lax.ppermute(lax.slice_in_dim(block, block.shape[dim] - width, None, axis...  24.4 us
    unnamed x20, other arithmetic  23.7 us
    ppermute x4, starting transfers between devices, padded_2(): lax.ppermute(last, axis, up)  22.9 us
    ppermute x4, waiting for transfers between devices, padded_2(): lax.ppermute(leading, axis, [(b, a) for a, b in up])  14 us
    ppermute x4, waiting for transfers between devices, extended(): lax.ppermute(lax.slice_in_dim(block, 0, width, axis=dim), axis, backward)  10.9 us
    ppermute x4, starting transfers between devices, padded_2(): lax.ppermute(leading, axis, [(b, a) for a, b in up])  9.12 us
    ppermute x4, starting transfers between devices, extended(): lax.ppermute(lax.slice_in_dim(block, 0, width, axis=dim), axis, backward)  8.35 us
    concatenate x3, other arithmetic, extended(): block = jnp.concatenate([low, block, high], axis=dim)  4.72 us
  transfers between devices with their start and end apart: 16, of which 5 were waited for; matrix products, arithmetic and copies ran while one was open for 4% of the time, Pallas kernels for 0%

commit v1 on v0

v1 whole, which is shorter than its diff:
```python
import functools

import jax
import jax.numpy as jnp
from jax import lax
from jax.experimental import pallas as pl
from jax.experimental.pallas import tpu as pltpu
from jax.sharding import PartitionSpec as P

STEPS = 2
TIME_STEP = 0.1
MESH = pl.DeviceIdType.MESH
NX, NY, NZ = 32, 8, 128
PITCH = 24
EXT = (NX + 4) * PITCH
TILES = 4

WEIGHT = {"F": {1: 27.0, 0: -27.0, 2: -1.0, -1: 1.0}, "B": {0: 27.0, -1: -27.0, 1: -1.0, -2: 1.0}}
LOW = {"F": (-1,), "B": (-2, -1)}
HIGH = {"F": (0, 1), "B": (0,)}
FORCE_X = ((0, "F"), (3, "B"), (4, "B"))
FORCE_Y = ((3, "B"), (1, "F"), (5, "B"))
FORCE_Z = ((4, "B"), (5, "B"), (2, "F"))
FLOW_X = ((0, "B"), (1, "F"), (2, "F"))
FLOW_Y = ((0, "F"), (1, "B"), (2, "F"))
FLOW_Z = ((0, "F"), (1, "F"), (2, "B"))


def layers(table, side):
    return [(field, layer) for field, kind in table for layer in side[kind]]


STRESS_Y = (layers(FORCE_Y, HIGH), layers(FORCE_Y, LOW))
STRESS_X = (layers(FORCE_X, HIGH), layers(FORCE_X, LOW))
FLOW_SENT_Y = (layers(FLOW_Y, HIGH), layers(FLOW_Y, LOW))
FLOW_SENT_X = (layers(FLOW_X, HIGH), layers(FLOW_X, LOW))
LIGHT = ((0, 1), (-2, -1))

YS, YP, XS, XV = range(4)
COUNTS = {
    YS: tuple(len(STRESS_Y[d]) for d in (0, 1)),
    YP: tuple(len(FLOW_SENT_Y[d]) for d in (0, 1)),
    XS: tuple(len(STRESS_X[d]) for d in (0, 1)),
    XV: tuple(len(FLOW_SENT_X[d]) for d in (0, 1)),
}


def message_rows(step, kind, direction):
    count = COUNTS[kind][direction]
    if kind == YS and step == 0:
        count += 2
    return count * (NX if kind in (YS, YP) else NY)


MESSAGES = [(s, k, d) for s in range(STEPS) for k in range(4) for d in (0, 1)]


def kernel(
    velocity,
    stress,
    lame_hbm,
    modulus_hbm,
    buoyancy_hbm,
    zone_hbm,
    eligible_hbm,
    cohesion_hbm,
    friction_hbm,
    cell_hbm,
    moment_hbm,
    velocity_out,
    stress_out,
    s_in,
    v_in,
    lame,
    modulus,
    buoyancy,
    zone,
    eligible,
    cohesion,
    friction,
    cell,
    moment,
    s_ext,
    v_ext,
    strength,
    slope,
    inject,
    v_res,
    s_res,
    *rest,
):
    sent = dict(zip(MESSAGES, rest[: len(MESSAGES)]))
    got = dict(zip(MESSAGES, rest[len(MESSAGES) : 2 * len(MESSAGES)]))
    load_sem, store_sem, send_sem, recv_sem = rest[2 * len(MESSAGES) :]
    gx, gy = lax.axis_index("gx"), lax.axis_index("gy")
    size_x, size_y = lax.axis_size("gx"), lax.axis_size("gy")

    there = {"x": (gx > 0, gx < size_x - 1), "y": (gy > 0, gy < size_y - 1)}
    target = {
        "x": ({"gx": gx - 1}, {"gx": gx + 1}),
        "y": ({"gy": gy - 1}, {"gy": gy + 1}),
    }

    barrier = pltpu.get_barrier_semaphore()
    for axis in "yx":
        for d in (0, 1):

            @pl.when(there[axis][d])
            def _():
                pl.semaphore_signal(
                    barrier, inc=1, device_id=target[axis][d], device_id_type=MESH
                )

    loads = [
        pltpu.make_async_copy(a, b, load_sem.at[i])
        for i, (a, b) in enumerate(
            (
                (stress, s_in),
                (buoyancy_hbm, buoyancy),
                (velocity, v_in),
                (zone_hbm, zone),
                (eligible_hbm, eligible),
                (lame_hbm, lame),
                (modulus_hbm, modulus),
                (cohesion_hbm, cohesion),
                (friction_hbm, friction),
                (cell_hbm, cell),
                (moment_hbm, moment),
            )
        )
    ]
    for load in loads:
        load.start()

    def axis_of(kind):
        return "y" if kind in (YS, YP) else "x"

    def remote(step, kind, d):
        at = MESSAGES.index((step, kind, d))
        return pltpu.make_async_remote_copy(
            src_ref=sent[step, kind, d],
            dst_ref=got[step, kind, d],
            send_sem=send_sem.at[at],
            recv_sem=recv_sem.at[at],
            device_id=target[axis_of(kind)][d],
            device_id_type=MESH,
        )

    def send(step, kind):
        for d in (0, 1):

            @pl.when(there[axis_of(kind)][d])
            def _():
                remote(step, kind, d).start()

    def receive(step, kind):
        for d in (0, 1):

            @pl.when(there[axis_of(kind)][1 - d])
            def _():
                remote(step, kind, d).wait_recv()

    for axis in "xy":
        for d in (0, 1):

            @pl.when(jnp.logical_not(there[axis][1 - d]))
            def _():
                for step, kind, way in MESSAGES:
                    if way == d and axis_of(kind) == axis:
                        ref = got[step, kind, way]
                        ref[...] = jnp.zeros(ref.shape, jnp.float32)

    zero = jnp.zeros((NY, NZ), jnp.float32)
    for field in (0, 3, 4):
        for x in (-2, -1, NX, NX + 1):
            s_ext[field, pl.ds((x + 2) * PITCH + NY, NY), :] = zero

    def clear(x, _):
        for field in (1, 3, 5):
            for offset in (0, 2 * NY):
                start = pl.multiple_of((x + 2) * PITCH + offset, NY)
                s_ext[field, pl.ds(start, NY), :] = zero
        return _

    lax.fori_loop(0, NX, clear, 0)

    lane = lax.broadcasted_iota(jnp.int32, (NY, NZ), 1)
    keep = {1: lane < NZ - 1, 2: lane < NZ - 2, -1: lane >= 1, -2: lane >= 2}

    def weighted(terms):
        total = None
        for weight, value in terms:
            if weight < 0 and total is not None:
                total = total - (value if weight == -1.0 else -weight * value)
            else:
                value = value if weight == 1.0 else weight * value
                total = value if total is None else total + value
        return total

    def spread(kind, at):
        if kind == "F":
            return 27.0 * (at(1) - at(0)) - (at(2) - at(-1))
        return 27.0 * (at(0) - at(-1)) - (at(1) - at(-2))

    def along_x(ref, field, kind, base):
        return spread(
            kind,
            lambda o: ref[field, pl.ds(pl.multiple_of(base + o * PITCH, NY), NY), :],
        )

    def along_y(ref, field, kind, base):
        return spread(
            kind,
            lambda o: ref[
                field, pl.ds(pl.multiple_of(base, NY) if o == 0 else base + o, NY), :
            ],
        )

    def along_z(ref, field, kind, base):
        value = ref[field, pl.ds(pl.multiple_of(base, NY), NY), :]

        def at(o):
            if o == 0:
                return value
            return jnp.where(keep[o], pltpu.roll(value, (-o) % NZ, 1), 0.0)

        return spread(kind, at)

    def place(x):
        return pl.multiple_of(x * NY, NY), (x + 2) * PITCH + NY

    def columns(row):
        return pl.ds(2 * PITCH + NY + row, NX, stride=PITCH)

    def part(ref, at, rows):
        return ref[pl.ds(at * rows, rows), :]


    def pack_stress(step):
        for d in (0, 1):
            base = NY if d else 0
            out = sent[step, YS, d]
            for at, (field, layer) in enumerate(STRESS_Y[d]):
                if step == 0:
                    value = s_in[field, pl.ds(base + layer, NX, stride=NY), :]
                else:
                    value = s_ext[field, columns(base + layer), :]
                out[pl.ds(at * NX, NX), :] = value
            if step == 0:
                for at, layer in enumerate(LIGHT[d]):
                    out[pl.ds((len(STRESS_Y[d]) + at) * NX, NX), :] = buoyancy[
                        pl.ds(base + layer, NX, stride=NY), :
                    ]
            base = NX if d else 0
            out = sent[step, XS, d]
            for at, (field, layer) in enumerate(STRESS_X[d]):
                x = base + layer
                if step == 0:
                    value = s_in[field, pl.ds(x * NY, NY), :]
                else:
                    value = s_ext[field, pl.ds((x + 2) * PITCH + NY, NY), :]
                out[pl.ds(at * NY, NY), :] = value

    def extend(k, _):
        for j in range(TILES):
            row, base = place(k * TILES + j)
            for field in range(6):
                s_ext[field, pl.ds(pl.multiple_of(base, NY), NY), :] = s_in[
                    field, pl.ds(row, NY), :
                ]
        return _

    def move(step):
        def body(k, _):
            for j in range(TILES):
                row, base = place(k * TILES + j)
                light = (TIME_STEP / 24.0) * buoyancy[pl.ds(row, NY), :]
                main = pl.ds(pl.multiple_of(base, NY), NY)
                for c in range(3):
                    force = along_x(s_ext, *FORCE_X[c], base)
                    force += along_y(s_ext, *FORCE_Y[c], base)
                    force += along_z(s_ext, *FORCE_Z[c], base)
                    old = v_in[c, pl.ds(row, NY), :] if step == 0 else v_ext[c, main, :]
                    v_ext[c, main, :] = old + light * force
            return _

        lax.fori_loop(0, NX // TILES, body, 0)

    def beyond(kind, low, i, count):
        if low:
            return [(WEIGHT[kind][r - i], r) for r in LOW[kind] if r - i in WEIGHT[kind]]
        return [
            (WEIGHT[kind][count + r - i], r) for r in HIGH[kind] if count + r - i in WEIGHT[kind]
        ]

    def mend_x(step):
        for low in (True, False):
            d = 1 if low else 0
            halo = got[step, XS, d]
            for i in (0, 1) if low else (NX - 2, NX - 1):
                light = (TIME_STEP / 24.0) * buoyancy[pl.ds(i * NY, NY), :]
                for c, (field, kind) in enumerate(FORCE_X):
                    terms = beyond(kind, low, i, NX)
                    if terms:
                        main = pl.ds((i + 2) * PITCH + NY, NY)
                        v_ext[c, main, :] += light * weighted(
                            [
                                (w, part(halo, STRESS_X[d].index((field, r)), NY))
                                for w, r in terms
                            ]
                        )

    def pack_flow_y(step):
        for d in (0, 1):
            base = NY if d else 0
            for at, (c, layer) in enumerate(FLOW_SENT_Y[d]):
                sent[step, YP, d][pl.ds(at * NX, NX), :] = v_ext[c, columns(base + layer), :]

    def mend_y(step):
        for low in (True, False):
            d = 1 if low else 0
            halo = got[step, YS, d]
            mine = sent[0, YS, 1 - d]
            for at, layer in enumerate(LIGHT[1 - d]):
                i = layer if low else NY + layer
                light = (TIME_STEP / 24.0) * part(mine, len(STRESS_Y[1 - d]) + at, NX)
                for c, (field, kind) in enumerate(FORCE_Y):
                    terms = beyond(kind, low, i, NY)
                    if terms:
                        v_ext[c, columns(i), :] += light * weighted(
                            [
                                (w, part(halo, STRESS_Y[d].index((field, r)), NX))
                                for w, r in terms
                            ]
                        )

    def pack_flow_x(step):
        for d in (0, 1):
            base = NX if d else 0
            for at, (c, layer) in enumerate(FLOW_SENT_X[d]):
                sent[step, XV, d][pl.ds(at * NY, NY), :] = v_ext[
                    c, pl.ds((base + layer + 2) * PITCH + NY, NY), :
                ]

    def finish_y(step):
        for low in (True, False):
            d = 1 if low else 0
            flow = got[step, YP, d]
            first = got[0, YS, d]
            own = sent[step, YS, 1 - d]
            for at, (c, layer) in enumerate(FLOW_SENT_Y[d]):
                light = (TIME_STEP / 24.0) * part(
                    first, len(STRESS_Y[d]) + LIGHT[d].index(layer), NX
                )
                field, kind = FORCE_Y[c]
                side = HIGH[kind] if low else LOW[kind]
                terms = [
                    (WEIGHT[kind][j - layer], part(own, STRESS_Y[1 - d].index((field, j)), NX))
                    for j in side
                    if j - layer in WEIGHT[kind]
                ]
                value = part(flow, at, NX)
                if terms:
                    value = value + light * weighted(terms)
                v_ext[c, columns(layer if low else NY + layer), :] = value

    def finish_x(step):
        for low in (True, False):
            d = 1 if low else 0
            for at, (c, layer) in enumerate(FLOW_SENT_X[d]):
                x = layer if low else NX + layer
                v_ext[c, pl.ds((x + 2) * PITCH + NY, NY), :] = part(got[step, XV, d], at, NY)

    def stress_layer(step, x):
        row, base = place(x)
        main = pl.ds(pl.multiple_of(base, NY), NY)
        here = pl.ds(row, NY)
        mu = (TIME_STEP / 24.0) * modulus[here, :]
        lam = (TIME_STEP / 24.0) * lame[here, :]
        e_x = along_x(v_ext, 0, "B", base)
        e_y = along_y(v_ext, 1, "B", base)
        e_z = along_z(v_ext, 2, "B", base)
        dilation = lam * (e_x + e_y + e_z)
        twice = mu + mu
        rates = (
            dilation + twice * e_x,
            dilation + twice * e_y,
            dilation + twice * e_z,
            mu * (along_y(v_ext, 0, "F", base) + along_x(v_ext, 1, "F", base)),
            mu * (along_z(v_ext, 0, "F", base) + along_x(v_ext, 2, "F", base)),
            mu * (along_z(v_ext, 1, "F", base) + along_y(v_ext, 2, "F", base)),
        )
        s = [s_ext[f, main, :] + (rates[f] + inject[f, here, :]) for f in range(6)]
        pressure = (s[0] + s[1] + s[2]) * (1.0 / 3.0)
        d = [s[f] - pressure for f in range(3)]
        second = 0.5 * (d[0] * d[0] + d[1] * d[1] + d[2] * d[2])
        second = second + s[3] * s[3] + s[4] * s[4] + s[5] * s[5]
        limit = jnp.maximum(strength[here, :] - pressure * slope[here, :], 0.0)
        ratio = limit * lax.rsqrt(jnp.maximum(second, 0.0625))
        factor = jnp.where(eligible[here, :] == 1, jnp.minimum(ratio, 1.0), 1.0)
        new = [pressure + factor * d[f] for f in range(3)] + [factor * s[f] for f in (3, 4, 5)]
        for f in range(6):
            if step == STEPS - 1:
                s_res[f, here, :] = new[f]
            else:
                s_ext[f, main, :] = new[f]

    def deform(step, start, stride, steps):
        def body(k, _):
            for j in range(2):
                stress_layer(step, start + k * stride + j)
            return _

        lax.fori_loop(0, steps, body, 0)

    def prepare():
        row = lax.broadcasted_iota(jnp.int32, (NY, NZ), 0)
        total_y = size_y * NY
        corner = ((gx * NX) * total_y + gy * NY) * NZ
        within = row * NZ + lane

        def body(x, _):
            here = pl.ds(pl.multiple_of(x * NY, NY), NY)
            which = zone[here, :]
            coh = jnp.full((NY, NZ), cohesion[0], jnp.float32)
            fri = jnp.full((NY, NZ), friction[0], jnp.float32)
            for z in range(1, 8):
                hit = which == z
                coh = jnp.where(hit, cohesion[z], coh)
                fri = jnp.where(hit, friction[z], fri)
            strength[here, :] = coh * jnp.sqrt(1.0 - fri * fri)
            slope[here, :] = fri
            index = within + (corner + x * (total_y * NZ))
            sums = [zero] * 6
            for source in range(16):
                hit = index == cell[source]
                for f in range(6):
                    sums[f] = sums[f] + jnp.where(hit, TIME_STEP * moment[f, source], 0.0)
            for f in range(6):
                inject[f, here, :] = sums[f]
            return _

        lax.fori_loop(0, NX, body, 0)


    for load in loads[:2]:
        load.wait()
    pack_stress(0)
    expected = sum(t.astype(jnp.int32) for axis in "xy" for t in there[axis])
    pl.semaphore_wait(barrier, expected)
    stores = []
    for step in range(STEPS):
        if step:
            pack_stress(step)
        send(step, YS)
        send(step, XS)
        if step == 0:
            lax.fori_loop(0, NX // TILES, extend, 0)
            loads[2].wait()
        move(step)
        receive(step, XS)
        mend_x(step)
        pack_flow_y(step)
        send(step, YP)
        if step == 0:
            for load in loads[3:]:
                load.wait()
            prepare()
        receive(step, YS)
        mend_y(step)
        pack_flow_x(step)
        send(step, XV)
        if step == STEPS - 1:

            def keep_flow(k, _):
                for j in range(TILES):
                    row, base = place(k * TILES + j)
                    for c in range(3):
                        v_res[c, pl.ds(row, NY), :] = v_ext[
                            c, pl.ds(pl.multiple_of(base, NY), NY), :
                        ]
                return _

            lax.fori_loop(0, NX // TILES, keep_flow, 0)
            store = pltpu.make_async_copy(v_res, velocity_out, store_sem.at[0])
            store.start()
            stores.append(store)
        receive(step, YP)
        finish_y(step)
        deform(step, 2, 2, (NX - 4) // 2)
        if step == STEPS - 1:
            inner = pl.ds(2 * NY, (NX - 4) * NY)
            store = pltpu.make_async_copy(
                s_res.at[:, inner], stress_out.at[:, inner], store_sem.at[1]
            )
            store.start()
            stores.append(store)
        receive(step, XV)
        finish_x(step)
        deform(step, 0, NX - 2, 2)
    for at, start in ((2, 0), (3, (NX - 2) * NY)):
        edge = pl.ds(start, 2 * NY)
        store = pltpu.make_async_copy(s_res.at[:, edge], stress_out.at[:, edge], store_sem.at[at])
        store.start()
        stores.append(store)
    for store in stores:
        store.wait()
    for step, kind, d in MESSAGES:

        @pl.when(there[axis_of(kind)][d])
        def _():
            remote(step, kind, d).wait_send()


def on_device(velocity, stress, lame, modulus, buoyancy, zone, eligible, *tables):
    rows = NX * NY
    flat = [a.reshape(a.shape[:-3] + (rows, NZ)) for a in (velocity, stress, lame, modulus, buoyancy, zone, eligible)]
    f32 = jnp.float32
    hbm = pl.BlockSpec(memory_space=pl.ANY)
    buffers = [
        pltpu.VMEM((message_rows(*m), NZ), f32) for m in MESSAGES
    ]
    block = pltpu.VMEM((rows, NZ), f32)
    whole = pltpu.VMEM((rows, NZ), jnp.int32)
    v, s = pl.pallas_call(
        kernel,
        out_shape=(
            jax.ShapeDtypeStruct((3, rows, NZ), f32),
            jax.ShapeDtypeStruct((6, rows, NZ), f32),
        ),
        in_specs=[hbm] * 11,
        out_specs=(hbm, hbm),
        scratch_shapes=[
            pltpu.VMEM((6, rows, NZ), f32),
            pltpu.VMEM((3, rows, NZ), f32),
            block,
            block,
            block,
            whole,
            whole,
            pltpu.SMEM((8,), f32),
            pltpu.SMEM((8,), f32),
            pltpu.SMEM((16,), jnp.int32),
            pltpu.SMEM((6, 16), f32),
            pltpu.VMEM((6, EXT, NZ), f32),
            pltpu.VMEM((3, EXT, NZ), f32),
            block,
            block,
            pltpu.VMEM((6, rows, NZ), f32),
            pltpu.VMEM((3, rows, NZ), f32),
            pltpu.VMEM((6, rows, NZ), f32),
            *buffers,
            *buffers,
            pltpu.SemaphoreType.DMA((11,)),
            pltpu.SemaphoreType.DMA((4,)),
            pltpu.SemaphoreType.DMA((len(MESSAGES),)),
            pltpu.SemaphoreType.DMA((len(MESSAGES),)),
        ],
        compiler_params=pltpu.CompilerParams(collective_id=0, has_side_effects=True),
    )(*flat, *tables)
    return v.reshape(velocity.shape), s.reshape(stress.shape)


def solution(mesh):
    wide, field, table = P(None, "gx", "gy", None), P("gx", "gy", None), P()
    return jax.shard_map(
        on_device,
        mesh=mesh,
        in_specs=(wide, wide) + (field,) * 5 + (table,) * 4,
        out_specs=(wide, wide),
        check_vma=False,
    )
```

time: 137 us -> 46 us (0.34)
  the two profiles are of different devices: /device:TPU:127 before, /device:TPU:383 now
where the time goes in v1:
time: 46 us; the launch traced here: 45.8 us
  Pallas kernels  42.5 us (92%)
  local copies, waits for them, and re-layouts  2.72 us (6%)
  between operations  0.65 us (1%)
    pallas_call x1, Pallas kernels, on_device(): pl.pallas_call(kernel, out_shape=(jax.ShapeDtypeStruct((3, rows, NZ), f32...  42.5 us
    unnamed x4, local copies, waits for them, and re-layouts  2.72 us

profile of v1, /device:TPU:383, one launch (start us, length us, event | category | flops | bytes accessed | tf_op | source)
XLA Modules:
  0.0 45.8 jit_solution(16409381361149287832)
XLA Ops:
  0.6 42.5 %shard_map.122 = (f32[3,256,128]{2,1,0:T(8,128)}, f32[6,256,128]{2,1,0:T(8,128)}) custom-call(f32[3,256,128]{2,1,0:T(8,128)} %bitcast.12, f32[6,256,128]{2,1,0:T(8,128)} %bitcast.10, f32[256,128]{1,0:T(8,128)} %bitcast.13, f32[256,128]{1,0:T(8,128)} %bitcast.14, f32[256,128]{1,0:T(8,128)} %bitcast.15, s32[256,128]{1,0:T(8,128)} %bitcast.16, ...), custom_call_target="tpu_custom_call" | custom-call | tf_op jit(solution)/shard_map/pallas_call | solution.py:525
  43.1 0.0 copy-start
  43.1 1.8 %copy.15 = f32[3,32,8,128]{3,2,1,0:T(8,128)} copy(f32[3,32,8,128]{3,2,1,0:T(8,128)} %bitcast.11) | data formatting | bytes 786432
  45.0 0.0 copy-done
  45.0 0.9 %copy.16 = f32[6,32,8,128]{3,2,1,0:T(8,128)} copy(f32[6,32,8,128]{3,2,1,0:T(8,128)S(1)} %bitcast.9) | data formatting | bytes 1572864
Async XLA Ops:
  43.1 1.9 %copy-start = (f32[6,256,128]{2,1,0:T(8,128)S(1)}, f32[6,256,128]{2,1,0:T(8,128)}, u32[]{:S(2)}) copy-start(f32[6,256,128]{2,1,0:T(8,128)} %get-tuple-element.5) | copy-start | bytes 2359300

commit v2 on v1

--- a/solution.py
+++ b/solution.py
@@ -36,23 +36,70 @@
 FLOW_SENT_X = (layers(FLOW_X, HIGH), layers(FLOW_X, LOW))
 LIGHT = ((0, 1), (-2, -1))
 
-YS, YP, XS, XV = range(4)
+YS, YP, XS, XP, CORNER = range(5)
 COUNTS = {
     YS: tuple(len(STRESS_Y[d]) for d in (0, 1)),
     YP: tuple(len(FLOW_SENT_Y[d]) for d in (0, 1)),
     XS: tuple(len(STRESS_X[d]) for d in (0, 1)),
-    XV: tuple(len(FLOW_SENT_X[d]) for d in (0, 1)),
+    XP: tuple(len(FLOW_SENT_X[d]) for d in (0, 1)),
 }
 
 
+def beyond(kind, low, i, count):
+    if low:
+        return [(WEIGHT[kind][r - i], r) for r in LOW[kind] if r - i in WEIGHT[kind]]
+    return [(WEIGHT[kind][count + r - i], r) for r in HIGH[kind] if count + r - i in WEIGHT[kind]]
+
+
+def corner(direction):
+    up_x, up_y = divmod(direction, 2)
+    base_x, base_y = NX * up_x, NY * up_y
+    along_y, along_x = [], []
+    for c, layer in FLOW_SENT_Y[up_y]:
+        field, kind = FORCE_X[c]
+        for i in (0, 1) if up_x else (NX - 2, NX - 1):
+            terms = beyond(kind, up_x, i, NX)
+            if terms:
+                along_y.append((c, layer, i, [(w, field, base_x + r, base_y + layer) for w, r in terms]))
+    for c, layer in FLOW_SENT_X[up_x]:
+        field, kind = FORCE_Y[c]
+        for i in (0, 1) if up_y else (NY - 2, NY - 1):
+            terms = beyond(kind, up_y, i, NY)
+            if terms:
+                along_x.append((c, layer, i, [(w, field, base_x + layer, base_y + r) for w, r in terms]))
+    return along_y, along_x
+
+
 def message_rows(step, kind, direction):
+    if kind == CORNER:
+        return 2 * NY
     count = COUNTS[kind][direction]
-    if kind == YS and step == 0:
+    if kind in (YS, XS) and step == 0:
         count += 2
     return count * (NX if kind in (YS, YP) else NY)
 
 
-MESSAGES = [(s, k, d) for s in range(STEPS) for k in range(4) for d in (0, 1)]
+RUN = 16
+SENDER = (0, RUN - 1)
+RELAY = ((RUN - 1, 3), (1, RUN - 3))
+PARTS = 1 + len(RELAY[0])
+
+
+def part_rows(step, kind, direction):
+    rows = message_rows(step, kind, direction)
+    each = rows // PARTS // NY * NY
+    cuts = [0] + [rows - each * (PARTS - 1 - p) for p in range(PARTS)]
+    return [pl.ds(a, b - a) for a, b in zip(cuts, cuts[1:])]
+
+
+MESSAGES = [
+    (s, k, d) for s in range(STEPS) for k in range(5) for d in range(4 if k == CORNER else 2)
+]
+PASSING = [(s, k) for s in range(STEPS) for k in (YS, YP)] if PARTS > 1 else []
+
+
+def passing_rows(step, kind):
+    return max(r.size for d in (0, 1) for r in part_rows(step, kind, d)[1:])
 
 
 def kernel(
@@ -85,25 +132,42 @@
     strength,
     slope,
     inject,
-    v_res,
-    s_res,
     *rest,
 ):
     sent = dict(zip(MESSAGES, rest[: len(MESSAGES)]))
     got = dict(zip(MESSAGES, rest[len(MESSAGES) : 2 * len(MESSAGES)]))
-    load_sem, store_sem, send_sem, recv_sem = rest[2 * len(MESSAGES) :]
+    rest = rest[2 * len(MESSAGES) :]
+    passing = dict(zip(PASSING, rest[: len(PASSING)]))
+    load_sem, send_sem, recv_sem, pass_sem, onward_sem = rest[len(PASSING) :]
     gx, gy = lax.axis_index("gx"), lax.axis_index("gy")
     size_x, size_y = lax.axis_size("gx"), lax.axis_size("gy")
 
     there = {"x": (gx > 0, gx < size_x - 1), "y": (gy > 0, gy < size_y - 1)}
+    there["xy"] = [a & b for a in there["x"] for b in there["y"]]
     target = {
         "x": ({"gx": gx - 1}, {"gx": gx + 1}),
         "y": ({"gy": gy - 1}, {"gy": gy + 1}),
+        "xy": [{"gx": gx + a, "gy": gy + b} for a in (-1, 1) for b in (-1, 1)],
     }
+    ways = {"x": (0, 1), "y": (0, 1), "xy": range(4)}
+
+    run, spot = gy // RUN, gy % RUN
+    beyond_run = (run > 0, run < size_y // RUN - 1)
+    crosses = [beyond_run[d] & (spot == SENDER[d]) for d in (0, 1)]
+    relays = [
+        (d, p, beyond_run[d] & (spot == RELAY[d][p - 1])) for d in (0, 1) for p in range(1, PARTS)
+    ]
 
     barrier = pltpu.get_barrier_semaphore()
-    for axis in "yx":
-        for d in (0, 1):
+    for d, _, mine in relays:
+
+        @pl.when(mine)
+        def _():
+            pl.semaphore_signal(
+                barrier, inc=1, device_id={"gy": run * RUN + SENDER[d]}, device_id_type=MESH
+            )
+    for axis in ("y", "xy", "x"):
+        for d in ways[axis]:
 
             @pl.when(there[axis][d])
             def _():
@@ -133,7 +197,7 @@
         load.start()
 
     def axis_of(kind):
-        return "y" if kind in (YS, YP) else "x"
+        return {YS: "y", YP: "y", XS: "x", XP: "x", CORNER: "xy"}[kind]
 
     def remote(step, kind, d):
         at = MESSAGES.index((step, kind, d))
@@ -146,24 +210,76 @@
             device_id_type=MESH,
         )
 
+    def cut(step, kind, d, p):
+        at = MESSAGES.index((step, kind, d))
+        rows = part_rows(step, kind, d)[p]
+        if p == 0:
+            into, sem, where = got[step, kind, d].at[rows], recv_sem.at[at], target["y"][d]
+        else:
+            into = passing[step, kind].at[pl.ds(0, rows.size)]
+            sem = pass_sem.at[PASSING.index((step, kind))]
+            where = {"gy": run * RUN + RELAY[d][p - 1]}
+        return pltpu.make_async_remote_copy(
+            src_ref=sent[step, kind, d].at[rows],
+            dst_ref=into,
+            send_sem=send_sem.at[at],
+            recv_sem=sem,
+            device_id=where,
+            device_id_type=MESH,
+        )
+
+    def onward(step, kind, d, p):
+        rows = part_rows(step, kind, d)[p]
+        return pltpu.make_async_remote_copy(
+            src_ref=passing[step, kind].at[pl.ds(0, rows.size)],
+            dst_ref=got[step, kind, d].at[rows],
+            send_sem=onward_sem.at[PASSING.index((step, kind))],
+            recv_sem=recv_sem.at[MESSAGES.index((step, kind, d))],
+            device_id={"gy": (run + (1 if d else -1)) * RUN + SENDER[1 - d]},
+            device_id_type=MESH,
+        )
+
+    def relay(step):
+        for d, p, mine in relays:
+
+            @pl.when(mine)
+            def _():
+                for kind in (YS, YP):
+                    cut(step, kind, d, p).wait_recv()
+                    onward(step, kind, d, p).start()
+
     def send(step, kind):
-        for d in (0, 1):
-
-            @pl.when(there[axis_of(kind)][d])
-            def _():
-                remote(step, kind, d).start()
+        axis = axis_of(kind)
+        for d in ways[axis]:
+            if axis != "y":
+
+                @pl.when(there[axis][d])
+                def _():
+                    remote(step, kind, d).start()
+
+            else:
+
+                @pl.when(there["y"][d] & jnp.logical_not(crosses[d]))
+                def _():
+                    remote(step, kind, d).start()
+
+                @pl.when(crosses[d])
+                def _():
+                    for p in reversed(range(PARTS)):
+                        cut(step, kind, d, p).start()
 
     def receive(step, kind):
-        for d in (0, 1):
-
-            @pl.when(there[axis_of(kind)][1 - d])
+        axis = axis_of(kind)
+        for d in ways[axis]:
+
+            @pl.when(there[axis][ways[axis][-1] - d])
             def _():
                 remote(step, kind, d).wait_recv()
 
-    for axis in "xy":
-        for d in (0, 1):
-
-            @pl.when(jnp.logical_not(there[axis][1 - d]))
+    for axis in ways:
+        for d in ways[axis]:
+
+            @pl.when(jnp.logical_not(there[axis][ways[axis][-1] - d]))
             def _():
                 for step, kind, way in MESSAGES:
                     if way == d and axis_of(kind) == axis:
@@ -260,6 +376,24 @@
                 else:
                     value = s_ext[field, pl.ds((x + 2) * PITCH + NY, NY), :]
                 out[pl.ds(at * NY, NY), :] = value
+            if step == 0:
+                for at, layer in enumerate(LIGHT[d]):
+                    out[pl.ds((len(STRESS_X[d]) + at) * NY, NY), :] = buoyancy[
+                        pl.ds((base + layer) * NY, NY), :
+                    ]
+
+    def pack_corner(step):
+        def row(field, x, y):
+            if step == 0:
+                return s_in[field, pl.ds(x * NY + y, 1), :]
+            return s_ext[field, pl.ds((x + 2) * PITCH + NY + y, 1), :]
+
+        for d in ways["xy"]:
+            for half, targets in enumerate(corner(d)):
+                for at, (_, _, _, terms) in enumerate(targets):
+                    sent[step, CORNER, d][pl.ds(half * NY + at, 1), :] = weighted(
+                        [(w, row(*where)) for w, *where in terms]
+                    )
 
     def extend(k, _):
         for j in range(TILES):
@@ -285,13 +419,6 @@
             return _
 
         lax.fori_loop(0, NX // TILES, body, 0)
-
-    def beyond(kind, low, i, count):
-        if low:
-            return [(WEIGHT[kind][r - i], r) for r in LOW[kind] if r - i in WEIGHT[kind]]
-        return [
-            (WEIGHT[kind][count + r - i], r) for r in HIGH[kind] if count + r - i in WEIGHT[kind]
-        ]
 
     def mend_x(step):
         for low in (True, False):
@@ -338,38 +465,55 @@
         for d in (0, 1):
             base = NX if d else 0
             for at, (c, layer) in enumerate(FLOW_SENT_X[d]):
-                sent[step, XV, d][pl.ds(at * NY, NY), :] = v_ext[
+                sent[step, XP, d][pl.ds(at * NY, NY), :] = v_ext[
                     c, pl.ds((base + layer + 2) * PITCH + NY, NY), :
                 ]
 
-    def finish_y(step):
+    row_of = lax.broadcasted_iota(jnp.int32, (NY, NZ), 0)
+
+    def scattered(step, d, half, c, layer, start):
+        total = None
+        for at, (field, which, i, _) in enumerate(corner(d)[half]):
+            if field == c and which == layer and start <= i < start + NY:
+                row = got[step, CORNER, d][pl.ds(half * NY + at, 1), :]
+                rest = zero if total is None else total
+                total = jnp.where(row_of == i - start, jnp.broadcast_to(row, (NY, NZ)), rest)
+        return [] if total is None else [(1.0, total)]
+
+    def finish(step, axis):
+        on_y = axis == "y"
+        tiles = NX // NY if on_y else 1
+        rows = NX if on_y else NY
+        moved, pushed = (YP, YS) if on_y else (XP, XS)
+        layers_sent, pulls = (FLOW_SENT_Y, STRESS_Y) if on_y else (FLOW_SENT_X, STRESS_X)
         for low in (True, False):
             d = 1 if low else 0
-            flow = got[step, YP, d]
-            first = got[0, YS, d]
-            own = sent[step, YS, 1 - d]
-            for at, (c, layer) in enumerate(FLOW_SENT_Y[d]):
-                light = (TIME_STEP / 24.0) * part(
-                    first, len(STRESS_Y[d]) + LIGHT[d].index(layer), NX
-                )
-                field, kind = FORCE_Y[c]
-                side = HIGH[kind] if low else LOW[kind]
-                terms = [
-                    (WEIGHT[kind][j - layer], part(own, STRESS_Y[1 - d].index((field, j)), NX))
-                    for j in side
-                    if j - layer in WEIGHT[kind]
-                ]
-                value = part(flow, at, NX)
-                if terms:
-                    value = value + light * weighted(terms)
-                v_ext[c, columns(layer if low else NY + layer), :] = value
-
-    def finish_x(step):
-        for low in (True, False):
-            d = 1 if low else 0
-            for at, (c, layer) in enumerate(FLOW_SENT_X[d]):
-                x = layer if low else NX + layer
-                v_ext[c, pl.ds((x + 2) * PITCH + NY, NY), :] = part(got[step, XV, d], at, NY)
+            flow, first, own = got[step, moved, d], got[0, pushed, d], sent[step, pushed, 1 - d]
+            for at, (c, layer) in enumerate(layers_sent[d]):
+                field, kind = (FORCE_Y if on_y else FORCE_X)[c]
+                for q in range(tiles):
+
+                    def tile(ref, index):
+                        return ref[pl.ds(index * rows + q * NY, NY), :]
+
+                    terms = [
+                        (WEIGHT[kind][j - layer], tile(own, pulls[1 - d].index((field, j))))
+                        for j in (HIGH[kind] if low else LOW[kind])
+                        if j - layer in WEIGHT[kind]
+                    ]
+                    for e in (0, 1):
+                        way = e * 2 + d if on_y else d * 2 + e
+                        terms += scattered(step, way, 0 if on_y else 1, c, layer, q * NY)
+                    value = tile(flow, at)
+                    if terms:
+                        light = tile(first, len(pulls[d]) + LIGHT[d].index(layer))
+                        value = value + (TIME_STEP / 24.0) * light * weighted(terms)
+                    if on_y:
+                        start = (2 + q * NY) * PITCH + NY + (layer if low else NY + layer)
+                        v_ext[c, pl.ds(start, NY, stride=PITCH), :] = value
+                    else:
+                        x = layer if low else NX + layer
+                        v_ext[c, pl.ds((x + 2) * PITCH + NY, NY), :] = value
 
     def stress_layer(step, x):
         row, base = place(x)
@@ -401,115 +545,109 @@
         new = [pressure + factor * d[f] for f in range(3)] + [factor * s[f] for f in (3, 4, 5)]
         for f in range(6):
             if step == STEPS - 1:
-                s_res[f, here, :] = new[f]
+                stress_out[f, here, :] = new[f]
+                if f < 3:
+                    velocity_out[f, here, :] = v_ext[f, main, :]
             else:
                 s_ext[f, main, :] = new[f]
 
-    def deform(step, start, stride, steps):
+    def deform(step):
         def body(k, _):
             for j in range(2):
-                stress_layer(step, start + k * stride + j)
+                stress_layer(step, k * 2 + j)
             return _
 
-        lax.fori_loop(0, steps, body, 0)
+        lax.fori_loop(0, NX // 2, body, 0)
 
     def prepare():
-        row = lax.broadcasted_iota(jnp.int32, (NY, NZ), 0)
         total_y = size_y * NY
-        corner = ((gx * NX) * total_y + gy * NY) * NZ
-        within = row * NZ + lane
-
-        def body(x, _):
-            here = pl.ds(pl.multiple_of(x * NY, NY), NY)
-            which = zone[here, :]
-            coh = jnp.full((NY, NZ), cohesion[0], jnp.float32)
-            fri = jnp.full((NY, NZ), friction[0], jnp.float32)
-            for z in range(1, 8):
-                hit = which == z
-                coh = jnp.where(hit, cohesion[z], coh)
-                fri = jnp.where(hit, friction[z], fri)
-            strength[here, :] = coh * jnp.sqrt(1.0 - fri * fri)
-            slope[here, :] = fri
-            index = within + (corner + x * (total_y * NZ))
-            sums = [zero] * 6
-            for source in range(16):
-                hit = index == cell[source]
-                for f in range(6):
-                    sums[f] = sums[f] + jnp.where(hit, TIME_STEP * moment[f, source], 0.0)
-            for f in range(6):
-                inject[f, here, :] = sums[f]
+        origin = ((gx * NX) * total_y + gy * NY) * NZ
+        within = row_of * NZ + lane
+
+        def body(k, _):
+            places = []
+            for j in range(TILES):
+                x = k * TILES + j
+                here = pl.ds(pl.multiple_of(x * NY, NY), NY)
+                which = zone[here, :]
+                coh = jnp.full((NY, NZ), cohesion[0], jnp.float32)
+                fri = jnp.full((NY, NZ), friction[0], jnp.float32)
+                for z in range(1, 8):
+                    hit = which == z
+                    coh = jnp.where(hit, cohesion[z], coh)
+                    fri = jnp.where(hit, friction[z], fri)
+                strength[here, :] = coh * jnp.sqrt(1.0 - fri * fri)
+                slope[here, :] = fri
+                places.append((here, within + (origin + x * (total_y * NZ))))
+            for group in ((0, 1, 2), (3, 4, 5)):
+                sums = [[zero] * len(group) for _ in places]
+                for source in range(16):
+                    moments = [moment[f, source] for f in group]
+                    for j, (here, index) in enumerate(places):
+                        hit = index == cell[source]
+                        for f, value in enumerate(moments):
+                            sums[j][f] = sums[j][f] + jnp.where(hit, value, 0.0)
+                for j, (here, index) in enumerate(places):
+                    for f, field in enumerate(group):
+                        inject[field, here, :] = TIME_STEP * sums[j][f]
             return _
 
-        lax.fori_loop(0, NX, body, 0)
-
-
+        lax.fori_loop(0, NX // TILES, body, 0)
+
+
+    for step in range(STEPS):
+        for d in ways["xy"]:
+            sent[step, CORNER, d][...] = jnp.zeros((2 * NY, NZ), jnp.float32)
     for load in loads[:2]:
         load.wait()
     pack_stress(0)
-    expected = sum(t.astype(jnp.int32) for axis in "xy" for t in there[axis])
+    pack_corner(0)
+    expected = sum(t.astype(jnp.int32) for axis in ways for t in there[axis])
+    expected += (PARTS - 1) * sum(c.astype(jnp.int32) for c in crosses)
     pl.semaphore_wait(barrier, expected)
-    stores = []
     for step in range(STEPS):
         if step:
             pack_stress(step)
         send(step, YS)
+        if step:
+            pack_corner(step)
+        send(step, CORNER)
         send(step, XS)
         if step == 0:
             lax.fori_loop(0, NX // TILES, extend, 0)
             loads[2].wait()
         move(step)
-        receive(step, XS)
-        mend_x(step)
         pack_flow_y(step)
         send(step, YP)
+        pack_flow_x(step)
+        send(step, XP)
         if step == 0:
             for load in loads[3:]:
                 load.wait()
             prepare()
+        relay(step)
+        receive(step, XS)
+        mend_x(step)
+        receive(step, XP)
         receive(step, YS)
         mend_y(step)
-        pack_flow_x(step)
-        send(step, XV)
-        if step == STEPS - 1:
-
-            def keep_flow(k, _):
-                for j in range(TILES):
-                    row, base = place(k * TILES + j)
-                    for c in range(3):
-                        v_res[c, pl.ds(row, NY), :] = v_ext[
-                            c, pl.ds(pl.multiple_of(base, NY), NY), :
-                        ]
-                return _
-
-            lax.fori_loop(0, NX // TILES, keep_flow, 0)
-            store = pltpu.make_async_copy(v_res, velocity_out, store_sem.at[0])
-            store.start()
-            stores.append(store)
+        receive(step, CORNER)
+        finish(step, "x")
         receive(step, YP)
-        finish_y(step)
-        deform(step, 2, 2, (NX - 4) // 2)
-        if step == STEPS - 1:
-            inner = pl.ds(2 * NY, (NX - 4) * NY)
-            store = pltpu.make_async_copy(
-                s_res.at[:, inner], stress_out.at[:, inner], store_sem.at[1]
-            )
-            store.start()
-            stores.append(store)
-        receive(step, XV)
-        finish_x(step)
-        deform(step, 0, NX - 2, 2)
-    for at, start in ((2, 0), (3, (NX - 2) * NY)):
-        edge = pl.ds(start, 2 * NY)
-        store = pltpu.make_async_copy(s_res.at[:, edge], stress_out.at[:, edge], store_sem.at[at])
-        store.start()
-        stores.append(store)
-    for store in stores:
-        store.wait()
+        finish(step, "y")
+        deform(step)
     for step, kind, d in MESSAGES:
 
         @pl.when(there[axis_of(kind)][d])
         def _():
             remote(step, kind, d).wait_send()
+
+    for d, p, mine in relays:
+
+        @pl.when(mine)
+        def _():
+            for step, kind in PASSING:
+                onward(step, kind, d, p).wait_send()
 
 
 def on_device(velocity, stress, lame, modulus, buoyancy, zone, eligible, *tables):
@@ -525,11 +663,11 @@
     v, s = pl.pallas_call(
         kernel,
         out_shape=(
-            jax.ShapeDtypeStruct((3, rows, NZ), f32),
-            jax.ShapeDtypeStruct((6, rows, NZ), f32),
+            pltpu.VMEM((3, rows, NZ), f32),
+            pltpu.VMEM((6, rows, NZ), f32),
         ),
         in_specs=[hbm] * 11,
-        out_specs=(hbm, hbm),
+        out_specs=(pl.BlockSpec(memory_space=pltpu.VMEM),) * 2,
         scratch_shapes=[
             pltpu.VMEM((6, rows, NZ), f32),
             pltpu.VMEM((3, rows, NZ), f32),
@@ -547,14 +685,14 @@
             block,
             block,
             pltpu.VMEM((6, rows, NZ), f32),
-            pltpu.VMEM((3, rows, NZ), f32),
-            pltpu.VMEM((6, rows, NZ), f32),
             *buffers,
             *buffers,
+            *[pltpu.VMEM((passing_rows(*m), NZ), f32) for m in PASSING],
             pltpu.SemaphoreType.DMA((11,)),
-            pltpu.SemaphoreType.DMA((4,)),
             pltpu.SemaphoreType.DMA((len(MESSAGES),)),
             pltpu.SemaphoreType.DMA((len(MESSAGES),)),
+            pltpu.SemaphoreType.DMA((max(len(PASSING), 1),)),
+            pltpu.SemaphoreType.DMA((max(len(PASSING), 1),)),
         ],
         compiler_params=pltpu.CompilerParams(collective_id=0, has_side_effects=True),
     )(*flat, *tables)

time: 46 us -> 36.1 us (0.78)
  the two profiles are of different devices: /device:TPU:383 before, /device:TPU:63 now
where the time goes in v2:
time: 36.1 us; the launch traced here: 35.9 us
  Pallas kernels  33.6 us (93%)
  local copies, waits for them, and re-layouts  1.63 us (5%)
  between operations  0.64 us (2%)
    pallas_call x1, Pallas kernels, on_device(): pl.pallas_call(kernel, out_shape=(pltpu.VMEM((3, rows, NZ), f32), pltpu.V...  33.6 us
    unnamed x2, local copies, waits for them, and re-layouts  1.63 us

profile of v2, /device:TPU:63, one launch (start us, length us, event | category | flops | bytes accessed | tf_op | source)
XLA Modules:
  0.0 35.9 jit_solution(9355176975338905209)
XLA Ops:
  0.6 33.6 %shard_map.122 = (f32[3,256,128]{2,1,0:T(8,128)S(1)}, f32[6,256,128]{2,1,0:T(8,128)S(1)}) custom-call(f32[3,256,128]{2,1,0:T(8,128)} %bitcast.12, f32[6,256,128]{2,1,0:T(8,128)} %bitcast.11, f32[256,128]{1,0:T(8,128)} %bitcast.13, f32[256,128]{1,0:T(8,128)} %bitcast.14, f32[256,128]{1,0:T(8,128)} %bitcast.15, s32[256,128]{1,0:T(8,128)} %bitcast.16, ...), custom_call_target="tpu_custom_call" | custom-call | tf_op jit(solution)/shard_map/pallas_call | solution.py:663
  34.3 0.7 %copy.15 = f32[3,32,8,128]{3,2,1,0:T(8,128)} copy(f32[3,32,8,128]{3,2,1,0:T(8,128)S(1)} %bitcast.10) | data formatting | bytes 786432
  35.0 0.9 %copy.16 = f32[6,32,8,128]{3,2,1,0:T(8,128)} copy(f32[6,32,8,128]{3,2,1,0:T(8,128)S(1)} %bitcast.9) | data formatting | bytes 1572864

commit v3 on v2

--- a/solution.py
+++ b/solution.py
@@ -14,6 +14,8 @@
 PITCH = 24
 EXT = (NX + 4) * PITCH
 TILES = 4
+BENT = 4
+DEEP = 16
 
 WEIGHT = {"F": {1: 27.0, 0: -27.0, 2: -1.0, -1: 1.0}, "B": {0: 27.0, -1: -27.0, 1: -1.0, -2: 1.0}}
 LOW = {"F": (-1,), "B": (-2, -1)}
@@ -81,14 +83,28 @@
 
 RUN = 16
 SENDER = (0, RUN - 1)
-RELAY = ((RUN - 1, 3), (1, RUN - 3))
+RELAY = ((14, 12, 2), (1, 3, 13))
 PARTS = 1 + len(RELAY[0])
+
+
+def shares(step, kind, direction):
+    if step == 0 and direction == 1:
+        return FIRST_UP
+    return LATER
+
+
+FIRST_UP = (0.4, 0.34, 0.26)
+LATER = (0.24, 0.24, 0.2)
 
 
 def part_rows(step, kind, direction):
     rows = message_rows(step, kind, direction)
-    each = rows // PARTS // NY * NY
-    cuts = [0] + [rows - each * (PARTS - 1 - p) for p in range(PARTS)]
+    sizes = [int(rows * share) // NY * NY for share in shares(step, kind, direction)]
+    if step == 0 and direction == 1:
+        sizes[0] = rows - sum(sizes[1:])
+    cuts = [0, rows - sum(sizes)]
+    for size in sizes:
+        cuts.append(cuts[-1] + size)
     return [pl.ds(a, b - a) for a, b in zip(cuts, cuts[1:])]
 
 
@@ -132,13 +148,15 @@
     strength,
     slope,
     inject,
+    in_depth,
     *rest,
 ):
     sent = dict(zip(MESSAGES, rest[: len(MESSAGES)]))
     got = dict(zip(MESSAGES, rest[len(MESSAGES) : 2 * len(MESSAGES)]))
     rest = rest[2 * len(MESSAGES) :]
     passing = dict(zip(PASSING, rest[: len(PASSING)]))
-    load_sem, send_sem, recv_sem, pass_sem, onward_sem = rest[len(PASSING) :]
+    turning = rest[len(PASSING)]
+    load_sem, send_sem, recv_sem, pass_sem, onward_sem, turn_sem, turned_sem, late_sem = rest[len(PASSING) + 1 :]
     gx, gy = lax.axis_index("gx"), lax.axis_index("gy")
     size_x, size_y = lax.axis_size("gx"), lax.axis_size("gy")
 
@@ -158,22 +176,57 @@
         (d, p, beyond_run[d] & (spot == RELAY[d][p - 1])) for d in (0, 1) for p in range(1, PARTS)
     ]
 
+    def hub(way):
+        return {"gx": gx + (1 if way // 2 else -1), "gy": run * RUN + RELAY[way % 2][0]}
+
+    turns = [
+        (way, beyond_run[way % 2] & (spot == RELAY[way % 2][0]) & there["x"][1 - way // 2])
+        for way in range(4)
+    ]
+    aways = [there["xy"][way] & crosses[way % 2] for way in range(4)]
+
+    origin = (gx == 0) & (gy == 0)
+    beside = {
+        "x": (gx == 1) & (gy == 0),
+        "y": (gx == 0) & (gy == 1),
+        "xy": (gx == 1) & (gy == 1),
+    }
+    greets, expects = {}, {}
+    for axis in ways:
+        last = ways[axis][-1]
+        greets[axis] = [there[axis][d] & jnp.logical_not(origin) for d in ways[axis]]
+        expects[axis] = list(there[axis])
+        expects[axis][0] = expects[axis][0] & jnp.logical_not(beside[axis])
+        if axis == "xy":
+            for d in ways[axis]:
+                greets[axis][d] = greets[axis][d] & jnp.logical_not(aways[d])
+                expects[axis][d] = expects[axis][d] & jnp.logical_not(aways[d])
+    greets["y"][0] = greets["y"][0] & jnp.logical_not(crosses[0])
+    expects["y"][1] = expects["y"][1] & jnp.logical_not(crosses[1])
+
     barrier = pltpu.get_barrier_semaphore()
+
+    def greet(when, where):
+        @pl.when(when)
+        def _():
+            pl.semaphore_signal(barrier, inc=1, device_id=where, device_id_type=MESH)
+
+    for place_up in RELAY[1]:
+        greet(crosses[0], {"gy": (run - 1) * RUN + place_up})
     for d, _, mine in relays:
-
-        @pl.when(mine)
-        def _():
-            pl.semaphore_signal(
-                barrier, inc=1, device_id={"gy": run * RUN + SENDER[d]}, device_id_type=MESH
-            )
+        greet(mine, {"gy": run * RUN + SENDER[d]})
+    for way, mine in turns:
+        greet(mine, {"gx": gx - (1 if way // 2 else -1), "gy": run * RUN + SENDER[way % 2]})
     for axis in ("y", "xy", "x"):
         for d in ways[axis]:
-
-            @pl.when(there[axis][d])
-            def _():
-                pl.semaphore_signal(
-                    barrier, inc=1, device_id=target[axis][d], device_id_type=MESH
-                )
+            greet(greets[axis][d], target[axis][d])
+
+    def amount(flags):
+        return sum(flag.astype(jnp.int32) for flag in flags)
+
+    expected = amount(f for axis in ways for f in expects[axis])
+    expected += (PARTS - 1) * amount(crosses) + amount(aways)
+    expected += amount(mine for d, _, mine in relays if d == 1)
 
     loads = [
         pltpu.make_async_copy(a, b, load_sem.at[i])
@@ -239,6 +292,36 @@
             device_id_type=MESH,
         )
 
+    def aside(step, d):
+        side = d // 2
+        return pltpu.make_async_remote_copy(
+            src_ref=sent[step, CORNER, d],
+            dst_ref=turning.at[step, side],
+            send_sem=send_sem.at[MESSAGES.index((step, CORNER, d))],
+            recv_sem=turn_sem.at[step, side],
+            device_id=hub(d),
+            device_id_type=MESH,
+        )
+
+    def turned(step, d):
+        side = d // 2
+        return pltpu.make_async_remote_copy(
+            src_ref=turning.at[step, side],
+            dst_ref=got[step, CORNER, d],
+            send_sem=turned_sem.at[step, side],
+            recv_sem=recv_sem.at[MESSAGES.index((step, CORNER, d))],
+            device_id={"gy": (run + (1 if d % 2 else -1)) * RUN + SENDER[1 - d % 2]},
+            device_id_type=MESH,
+        )
+
+    def turn(step):
+        for d, mine in turns:
+
+            @pl.when(mine)
+            def _():
+                aside(step, d).wait_recv()
+                turned(step, d).start()
+
     def relay(step):
         for d, p, mine in relays:
 
@@ -251,22 +334,39 @@
     def send(step, kind):
         axis = axis_of(kind)
         for d in ways[axis]:
-            if axis != "y":
-
-                @pl.when(there[axis][d])
+            now = there[axis][d]
+            if d == 0 and step == 0:
+                now = now & jnp.logical_not(beside[axis])
+            if axis == "x":
+
+                @pl.when(now)
                 def _():
                     remote(step, kind, d).start()
 
             else:
-
-                @pl.when(there["y"][d] & jnp.logical_not(crosses[d]))
+                across = aways[d] if axis == "xy" else crosses[d]
+
+                @pl.when(now & jnp.logical_not(across))
                 def _():
                     remote(step, kind, d).start()
 
-                @pl.when(crosses[d])
+                @pl.when(across)
                 def _():
-                    for p in reversed(range(PARTS)):
-                        cut(step, kind, d, p).start()
+                    if axis == "xy":
+                        aside(step, d).start()
+                    else:
+                        for p in reversed(range(PARTS)):
+                            if part_rows(step, kind, d)[p].size:
+                                cut(step, kind, d, p).start()
+
+    def send_origin():
+        for axis, kinds in (("y", (YS, YP)), ("xy", (CORNER,)), ("x", (XS, XP))):
+
+            @pl.when(beside[axis])
+            def _():
+                pl.semaphore_wait(late_sem, 1)
+                for kind in kinds:
+                    remote(0, kind, 0).start()
 
     def receive(step, kind):
         axis = axis_of(kind)
@@ -334,13 +434,22 @@
 
     def along_z(ref, field, kind, base):
         value = ref[field, pl.ds(pl.multiple_of(base, NY), NY), :]
-
-        def at(o):
-            if o == 0:
-                return value
-            return jnp.where(keep[o], pltpu.roll(value, (-o) % NZ, 1), 0.0)
-
-        return spread(kind, at)
+        return spread(kind, lambda o: turned_z(value, o))
+
+    def turned_z(value, o):
+        if o == 0:
+            return value
+        return jnp.where(keep[o], pltpu.roll(value, (-o) % NZ, 1), 0.0)
+
+    def depth(ref, table):
+        def body(k, _):
+            for j in range(DEEP):
+                row, base = place(k * DEEP + j)
+                for c, (field, kind) in enumerate(table):
+                    in_depth[c, pl.ds(row, NY), :] = along_z(ref, field, kind, base)
+            return _
+
+        lax.fori_loop(0, NX // DEEP, body, 0)
 
     def place(x):
         return pl.multiple_of(x * NY, NY), (x + 2) * PITCH + NY
@@ -413,7 +522,7 @@
                 for c in range(3):
                     force = along_x(s_ext, *FORCE_X[c], base)
                     force += along_y(s_ext, *FORCE_Y[c], base)
-                    force += along_z(s_ext, *FORCE_Z[c], base)
+                    force += in_depth[c, pl.ds(row, NY), :]
                     old = v_in[c, pl.ds(row, NY), :] if step == 0 else v_ext[c, main, :]
                     v_ext[c, main, :] = old + light * force
             return _
@@ -437,11 +546,38 @@
                             ]
                         )
 
+    def outflow(step, c, x, y, skip):
+        base = (x + 2) * PITCH + NY + y
+        inner = pl.ds(x * NY + y, NY, stride=NY) if skip > 1 else pl.ds(x * NY + y, NY)
+
+        def rows(ref, field, o):
+            at = pl.ds(base + o, NY, stride=skip) if skip > 1 else pl.ds(base + o, NY)
+            return ref[field, at, :]
+
+        field, kind = FORCE_X[c]
+        force = spread(kind, lambda o: rows(s_ext, field, o * PITCH))
+        field, kind = FORCE_Y[c]
+        force += spread(kind, lambda o: rows(s_ext, field, o))
+        field, kind = FORCE_Z[c]
+        value = rows(s_ext, field, 0)
+        force += spread(kind, lambda o: turned_z(value, o))
+        old = v_in[c, inner, :] if step == 0 else rows(v_ext, c, 0)
+        return old + (TIME_STEP / 24.0) * buoyancy[inner, :] * force
+
     def pack_flow_y(step):
         for d in (0, 1):
             base = NY if d else 0
             for at, (c, layer) in enumerate(FLOW_SENT_Y[d]):
-                sent[step, YP, d][pl.ds(at * NX, NX), :] = v_ext[c, columns(base + layer), :]
+                for q in range(NX // NY):
+                    sent[step, YP, d][pl.ds(at * NX + q * NY, NY), :] = outflow(
+                        step, c, q * NY, base + layer, PITCH
+                    )
+
+    def pack_flow_x(step):
+        for d in (0, 1):
+            base = NX if d else 0
+            for at, (c, layer) in enumerate(FLOW_SENT_X[d]):
+                sent[step, XP, d][pl.ds(at * NY, NY), :] = outflow(step, c, base + layer, 0, 1)
 
     def mend_y(step):
         for low in (True, False):
@@ -460,14 +596,6 @@
                                 for w, r in terms
                             ]
                         )
-
-    def pack_flow_x(step):
-        for d in (0, 1):
-            base = NX if d else 0
-            for at, (c, layer) in enumerate(FLOW_SENT_X[d]):
-                sent[step, XP, d][pl.ds(at * NY, NY), :] = v_ext[
-                    c, pl.ds((base + layer + 2) * PITCH + NY, NY), :
-                ]
 
     row_of = lax.broadcasted_iota(jnp.int32, (NY, NZ), 0)
 
@@ -523,7 +651,7 @@
         lam = (TIME_STEP / 24.0) * lame[here, :]
         e_x = along_x(v_ext, 0, "B", base)
         e_y = along_y(v_ext, 1, "B", base)
-        e_z = along_z(v_ext, 2, "B", base)
+        e_z = in_depth[2, here, :]
         dilation = lam * (e_x + e_y + e_z)
         twice = mu + mu
         rates = (
@@ -531,8 +659,8 @@
             dilation + twice * e_y,
             dilation + twice * e_z,
             mu * (along_y(v_ext, 0, "F", base) + along_x(v_ext, 1, "F", base)),
-            mu * (along_z(v_ext, 0, "F", base) + along_x(v_ext, 2, "F", base)),
-            mu * (along_z(v_ext, 1, "F", base) + along_y(v_ext, 2, "F", base)),
+            mu * (in_depth[0, here, :] + along_x(v_ext, 2, "F", base)),
+            mu * (in_depth[1, here, :] + along_y(v_ext, 2, "F", base)),
         )
         s = [s_ext[f, main, :] + (rates[f] + inject[f, here, :]) for f in range(6)]
         pressure = (s[0] + s[1] + s[2]) * (1.0 / 3.0)
@@ -553,15 +681,15 @@
 
     def deform(step):
         def body(k, _):
-            for j in range(2):
-                stress_layer(step, k * 2 + j)
+            for j in range(BENT):
+                stress_layer(step, k * BENT + j)
             return _
 
-        lax.fori_loop(0, NX // 2, body, 0)
+        lax.fori_loop(0, NX // BENT, body, 0)
 
     def prepare():
         total_y = size_y * NY
-        origin = ((gx * NX) * total_y + gy * NY) * NZ
+        first = ((gx * NX) * total_y + gy * NY) * NZ
         within = row_of * NZ + lane
 
         def body(k, _):
@@ -578,7 +706,7 @@
                     fri = jnp.where(hit, friction[z], fri)
                 strength[here, :] = coh * jnp.sqrt(1.0 - fri * fri)
                 slope[here, :] = fri
-                places.append((here, within + (origin + x * (total_y * NZ))))
+                places.append((here, within + (first + x * (total_y * NZ))))
             for group in ((0, 1, 2), (3, 4, 5)):
                 sums = [[zero] * len(group) for _ in places]
                 for source in range(16):
@@ -598,39 +726,57 @@
     for step in range(STEPS):
         for d in ways["xy"]:
             sent[step, CORNER, d][...] = jnp.zeros((2 * NY, NZ), jnp.float32)
-    for load in loads[:2]:
-        load.wait()
-    pack_stress(0)
-    pack_corner(0)
-    expected = sum(t.astype(jnp.int32) for axis in ways for t in there[axis])
-    expected += (PARTS - 1) * sum(c.astype(jnp.int32) for c in crosses)
-    pl.semaphore_wait(barrier, expected)
     for step in range(STEPS):
-        if step:
-            pack_stress(step)
+        if step == 0:
+            for load in loads[:2]:
+                load.wait()
+            lax.fori_loop(0, NX // TILES, extend, 0)
+            loads[2].wait()
+        pack_stress(step)
+        if step == 0:
+            pack_corner(step)
+            pack_flow_y(step)
+            pack_flow_x(step)
+            pl.semaphore_wait(barrier, expected)
+            for axis in ways:
+                up = ways[axis][-1]
+
+                @pl.when(origin & there[axis][up])
+                def _():
+                    pl.semaphore_signal(
+                        late_sem, inc=1, device_id=target[axis][up], device_id_type=MESH
+                    )
+
         send(step, YS)
         if step:
             pack_corner(step)
         send(step, CORNER)
         send(step, XS)
+        if step:
+            pack_flow_y(step)
+        send(step, YP)
+        if step:
+            pack_flow_x(step)
+        send(step, XP)
         if step == 0:
-            lax.fori_loop(0, NX // TILES, extend, 0)
-            loads[2].wait()
+            relay(step)
+            turn(step)
+        depth(s_ext, FORCE_Z)
         move(step)
-        pack_flow_y(step)
-        send(step, YP)
-        pack_flow_x(step)
-        send(step, XP)
         if step == 0:
             for load in loads[3:]:
                 load.wait()
             prepare()
-        relay(step)
+            send_origin()
+        else:
+            relay(step)
+            turn(step)
         receive(step, XS)
         mend_x(step)
         receive(step, XP)
         receive(step, YS)
         mend_y(step)
+        depth(v_ext, FLOW_Z)
         receive(step, CORNER)
         finish(step, "x")
         receive(step, YP)
@@ -642,12 +788,32 @@
         def _():
             remote(step, kind, d).wait_send()
 
+    for d, mine in turns:
+
+        @pl.when(mine)
+        def _():
+            for step in range(STEPS):
+                turned(step, d).wait_send()
+
     for d, p, mine in relays:
 
         @pl.when(mine)
         def _():
             for step, kind in PASSING:
                 onward(step, kind, d, p).wait_send()
+
+
+def write(velocity, stress, velocity_out, stress_out, sem):
+    copies = [
+        pltpu.make_async_copy(a.at[f], b.at[f], sem.at[at])
+        for at, (a, b, f) in enumerate(
+            [(velocity, velocity_out, f) for f in range(3)] + [(stress, stress_out, f) for f in range(6)]
+        )
+    ]
+    for copy in copies:
+        copy.start()
+    for copy in copies:
+        copy.wait()
 
 
 def on_device(velocity, stress, lame, modulus, buoyancy, zone, eligible, *tables):
@@ -685,17 +851,33 @@
             block,
             block,
             pltpu.VMEM((6, rows, NZ), f32),
+            pltpu.VMEM((3, rows, NZ), f32),
             *buffers,
             *buffers,
             *[pltpu.VMEM((passing_rows(*m), NZ), f32) for m in PASSING],
+            pltpu.VMEM((STEPS, 2, 2 * NY, NZ), f32),
             pltpu.SemaphoreType.DMA((11,)),
             pltpu.SemaphoreType.DMA((len(MESSAGES),)),
             pltpu.SemaphoreType.DMA((len(MESSAGES),)),
             pltpu.SemaphoreType.DMA((max(len(PASSING), 1),)),
             pltpu.SemaphoreType.DMA((max(len(PASSING), 1),)),
+            pltpu.SemaphoreType.DMA((STEPS, 2)),
+            pltpu.SemaphoreType.DMA((STEPS, 2)),
+            pltpu.SemaphoreType.REGULAR,
         ],
         compiler_params=pltpu.CompilerParams(collective_id=0, has_side_effects=True),
     )(*flat, *tables)
+    v, s = pl.pallas_call(
+        write,
+        out_shape=(
+            jax.ShapeDtypeStruct((3, rows, NZ), f32),
+            jax.ShapeDtypeStruct((6, rows, NZ), f32),
+        ),
+        in_specs=[hbm] * 2,
+        out_specs=(hbm, hbm),
+        scratch_shapes=[pltpu.SemaphoreType.DMA((9,))],
+        compiler_params=pltpu.CompilerParams(vmem_limit_bytes=1 << 20),
+    )(v, s)
     return v.reshape(velocity.shape), s.reshape(stress.shape)
 
 

time: 36.1 us -> 31.6 us (0.88)
  Pallas kernels: 33.6 us -> 30.8 us
  local copies, waits for them, and re-layouts: 1.63 us -> 0 us
    pallas_call x1, Pallas kernels: 33.6 us -> 29.7 us  [on_device(): pl.pallas_call(kernel, out_shape=(pltpu.VMEM((3, rows, NZ), f32), pltpu.V...]
    unnamed x2 -> x0, local copies, waits for them, and re-layouts: 1.63 us -> none
    pallas_call x0 -> x1, Pallas kernels: none -> 1.08 us  [on_device(): pl.pallas_call(write, out_shape=(jax.ShapeDtypeStruct((3, rows, NZ), f32)...]
where the time goes in v3:
time: 31.6 us; the launch traced here: 31.4 us
  Pallas kernels  30.8 us (97%)
  between operations  0.64 us (2%)
    pallas_call x1, Pallas kernels, on_device(): pl.pallas_call(kernel, out_shape=(pltpu.VMEM((3, rows, NZ), f32), pltpu.V...  29.7 us
    pallas_call x1, Pallas kernels, on_device(): pl.pallas_call(write, out_shape=(jax.ShapeDtypeStruct((3, rows, NZ), f32)...  1.08 us

profile of v3, /device:TPU:63, one launch (start us, length us, event | category | flops | bytes accessed | tf_op | source)
XLA Modules:
  0.0 31.4 jit_solution(10803940729524254301)
XLA Ops:
  0.6 29.7 %shard_map.122 = (f32[3,256,128]{2,1,0:T(8,128)S(1)}, f32[6,256,128]{2,1,0:T(8,128)S(1)}) custom-call(f32[3,256,128]{2,1,0:T(8,128)} %bitcast.10, f32[6,256,128]{2,1,0:T(8,128)} %bitcast.9, f32[256,128]{1,0:T(8,128)} %bitcast.11, f32[256,128]{1,0:T(8,128)} %bitcast.12, f32[256,128]{1,0:T(8,128)} %bitcast.13, s32[256,128]{1,0:T(8,128)} %bitcast.14, ...), custom_call_target="tpu_custom_call" | custom-call | tf_op jit(solution)/shard_map/pallas_call | solution.py:829
  30.3 1.1 %shard_map.123 = (f32[3,256,128]{2,1,0:T(8,128)}, f32[6,256,128]{2,1,0:T(8,128)}) custom-call(f32[3,256,128]{2,1,0:T(8,128)S(1)} %get-tuple-element.6.velocity, f32[6,256,128]{2,1,0:T(8,128)S(1)} %get-tuple-element.7.stress), custom_call_target="tpu_custom_call" | custom-call | tf_op jit(solution)/shard_map/pallas_call | solution.py:870

commit v4 on v3

--- a/solution.py
+++ b/solution.py
@@ -401,7 +401,11 @@
     lax.fori_loop(0, NX, clear, 0)
 
     lane = lax.broadcasted_iota(jnp.int32, (NY, NZ), 1)
-    keep = {1: lane < NZ - 1, 2: lane < NZ - 2, -1: lane >= 1, -2: lane >= 2}
+
+    def keep(o, rows):
+        at = lax.broadcasted_iota(jnp.int32, (rows, NZ), 1)
+        return at < NZ - o if o > 0 else at >= -o
+
 
     def weighted(terms):
         total = None
@@ -439,7 +443,7 @@
     def turned_z(value, o):
         if o == 0:
             return value
-        return jnp.where(keep[o], pltpu.roll(value, (-o) % NZ, 1), 0.0)
+        return jnp.where(keep(o, value.shape[0]), pltpu.roll(value, (-o) % NZ, 1), 0.0)
 
     def depth(ref, table):
         def body(k, _):
@@ -590,11 +594,15 @@
                 for c, (field, kind) in enumerate(FORCE_Y):
                     terms = beyond(kind, low, i, NY)
                     if terms:
-                        v_ext[c, columns(i), :] += light * weighted(
+                        value = v_ext[c, columns(i), :] + light * weighted(
                             [
                                 (w, part(halo, STRESS_Y[d].index((field, r)), NX))
                                 for w, r in terms
                             ]
+                        )
+                        v_ext[c, columns(i), :] = value
+                        in_depth[c, pl.ds(i, NX, stride=NY), :] = spread(
+                            FLOW_Z[c][1], lambda o: turned_z(value, o)
                         )
 
     row_of = lax.broadcasted_iota(jnp.int32, (NY, NZ), 0)
@@ -773,10 +781,10 @@
             turn(step)
         receive(step, XS)
         mend_x(step)
+        depth(v_ext, FLOW_Z)
         receive(step, XP)
         receive(step, YS)
         mend_y(step)
-        depth(v_ext, FLOW_Z)
         receive(step, CORNER)
         finish(step, "x")
         receive(step, YP)

time: 31.6 us -> 31.6 us (level)
  no operation moved by 1% of the time
where the time goes in v4:
time: 31.6 us; the launch traced here: 31.4 us
  Pallas kernels  30.8 us (97%)
  between operations  0.64 us (2%)
    pallas_call x1, Pallas kernels, on_device(): pl.pallas_call(kernel, out_shape=(pltpu.VMEM((3, rows, NZ), f32), pltpu.V...  29.7 us
    pallas_call x1, Pallas kernels, on_device(): pl.pallas_call(write, out_shape=(jax.ShapeDtypeStruct((3, rows, NZ), f32)...  1.08 us

profile of v4, /device:TPU:63, one launch (start us, length us, event | category | flops | bytes accessed | tf_op | source)
XLA Modules:
  0.0 31.4 jit_solution(554648946493758530)
XLA Ops:
  0.6 29.7 %shard_map.122 = (f32[3,256,128]{2,1,0:T(8,128)S(1)}, f32[6,256,128]{2,1,0:T(8,128)S(1)}) custom-call(f32[3,256,128]{2,1,0:T(8,128)} %bitcast.10, f32[6,256,128]{2,1,0:T(8,128)} %bitcast.9, f32[256,128]{1,0:T(8,128)} %bitcast.11, f32[256,128]{1,0:T(8,128)} %bitcast.12, f32[256,128]{1,0:T(8,128)} %bitcast.13, s32[256,128]{1,0:T(8,128)} %bitcast.14, ...), custom_call_target="tpu_custom_call" | custom-call | tf_op jit(solution)/shard_map/pallas_call | solution.py:837
  30.3 1.1 %shard_map.123 = (f32[3,256,128]{2,1,0:T(8,128)}, f32[6,256,128]{2,1,0:T(8,128)}) custom-call(f32[3,256,128]{2,1,0:T(8,128)S(1)} %get-tuple-element.6.velocity, f32[6,256,128]{2,1,0:T(8,128)S(1)} %get-tuple-element.7.stress), custom_call_target="tpu_custom_call" | custom-call | tf_op jit(solution)/shard_map/pallas_call | solution.py:878
